TPU v7x, 32 devices: a whole 2x2x4 slice. The times are simulated.
32 devices in a mesh: rows: 8 (over y, x, core), rep: 4 (over z).
Axes of the slice: x: 2, y: 2, z: 4, core: 2. Of those that a mesh axis runs over, the one named last changes fastest.
Arguments:
- maps: float32 [4, 4096, 4096], P('rep', 'rows'), may hold values from -12 to 12
- mask: int32 [4096, 4096], P('rows'), may hold values 0 or 1
- bins: int32 [4096, 4096], P(None, 'rows'), may hold values from 0 to 1023
Outputs:
- spectra: float32 [2, 3, 1024], replicated
All inputs are finite; a program needn't handle non-finite values. No bound on the sum of `mask` on one device may be relied on, other than what follows from the above.
Results may differ from a plain program's by a relative error of at most 0.0016.
Values sent between devices are 32-bit elements; how exact they have to be, the bound alone decides.
No kernel may reach another device: no remote copies, remote signals or barrier semaphores. Data moves between devices by JAX's collectives and lax.ppermute only.
A program may use at most 128 MiB of HBM per device.

v0:
```python
import math

import jax
import jax.numpy as jnp
from jax import lax
from jax.sharding import PartitionSpec as P

NBINS = 1024


precise = lax.Precision.HIGHEST


def partner(array, axis, distance):
    return lax.ppermute(array, axis, [(i, i ^ 1 << distance) for i in range(lax.axis_size(axis))])


def dft_table(count_a, count_b, period):
    first = lax.iota(jnp.int32, count_a)[:, None]
    second = lax.iota(jnp.int32, count_b)[None, :]
    angles = (first * second % period).astype(jnp.float32) * (2.0 * math.pi / period)
    return (jnp.cos(angles), -jnp.sin(angles))


def split_length(length):
    outer_len = 2 ** ((length.bit_length() - 1) // 2)
    return (outer_len, length // outer_len)


def complex_apply(form, real_part, imag_part, table_cos, table_sin):

    def product(left, right):
        return jnp.einsum(form, left, right, precision=precise)

    return (
        product(real_part, table_cos) - product(imag_part, table_sin),
        product(real_part, table_sin) + product(imag_part, table_cos),
    )


def twiddled(real_part, imag_part, table_cos, table_sin):
    return (
        real_part * table_cos - imag_part * table_sin,
        real_part * table_sin + imag_part * table_cos,
    )


def row_transform(values):
    count, length = values.shape
    outer_len, inner_len = split_length(length)
    outer_cos, outer_sin = dft_table(outer_len, outer_len, outer_len)
    inner_cos, inner_sin = dft_table(inner_len, inner_len, inner_len)
    turn_cos, turn_sin = dft_table(outer_len, inner_len, length)
    shaped = values.reshape(count, outer_len, inner_len)
    first_real = jnp.einsum("yan,ak->ykn", shaped, outer_cos, precision=precise)
    first_imag = jnp.einsum("yan,ak->ykn", shaped, outer_sin, precision=precise)
    mid_real, mid_imag = twiddled(first_real, first_imag, turn_cos, turn_sin)
    last_real, last_imag = complex_apply("ykn,nm->ymk", mid_real, mid_imag, inner_cos, inner_sin)
    return (last_real.reshape(count, length), last_imag.reshape(count, length))


def column_transform(pieces):
    real_part, imag_part = pieces
    length, groups, width = real_part.shape
    outer_len, inner_len = split_length(length)
    outer_cos, outer_sin = dft_table(outer_len, outer_len, outer_len)
    inner_cos, inner_sin = dft_table(inner_len, inner_len, inner_len)
    turn_cos, turn_sin = dft_table(outer_len, inner_len, length)
    shaped_real = real_part.reshape(outer_len, inner_len, groups, width)
    shaped_imag = imag_part.reshape(outer_len, inner_len, groups, width)
    first_real, first_imag = complex_apply(
        "anbc,ak->knbc", shaped_real, shaped_imag, outer_cos, outer_sin
    )
    mid_real, mid_imag = twiddled(
        first_real, first_imag, turn_cos[:, :, None, None], turn_sin[:, :, None, None]
    )
    last_real, last_imag = complex_apply("knbc,nm->mkbc", mid_real, mid_imag, inner_cos, inner_sin)
    return (last_real.reshape(length, groups, width), last_imag.reshape(length, groups, width))


def signed_float(indices, extent):
    return jnp.where(indices >= extent // 2, indices - extent, indices).astype(jnp.float32)


def band_terms(fields, freq_y, freq_x, bin_block, nbins_count, extent):
    q_real, q_imag, u_real, u_imag = fields
    radius = jnp.maximum(freq_x * freq_x + freq_y * freq_y, 1.0)
    cos_twice = (freq_x * freq_x - freq_y * freq_y) / radius
    sin_twice = 2.0 * freq_x * freq_y / radius
    e_real = cos_twice * q_real + sin_twice * u_real
    e_imag = cos_twice * q_imag + sin_twice * u_imag
    b_real = -sin_twice * q_real + cos_twice * u_real
    b_imag = -sin_twice * q_imag + cos_twice * u_imag
    inv_area = 1.0 / (extent * extent)
    powers = jnp.stack(
        [
            (e_real * e_real + e_imag * e_imag) * inv_area,
            (b_real * b_real + b_imag * b_imag) * inv_area,
            (e_real * b_real + e_imag * b_imag) * inv_area,
        ]
    ).astype(jnp.bfloat16)
    bit_count = nbins_count.bit_length() - 1
    high_count = 2 ** max(bit_count // 2 - 1, 0)
    low_count = nbins_count // high_count
    high_part = bin_block // low_count
    low_part = bin_block % low_count
    high_hot = (high_part[None] == lax.iota(jnp.int32, high_count)[:, None, None]).astype(
        jnp.bfloat16
    )
    weighted = (powers[:, None] * high_hot[None]).reshape(3 * high_count, -1)
    low_hot = (low_part[None] == lax.iota(jnp.int32, low_count)[:, None, None]).astype(jnp.bfloat16)
    low_hot = low_hot.reshape(low_count, -1)
    sums = lax.dot_general(
        weighted, low_hot, (((1,), (1,)), ((), ())), preferred_element_type=jnp.float32
    )
    return sums.reshape(3, nbins_count)


def on_device(maps, mask, bins):
    extent = bins.shape[0]
    columns = bins.shape[1]
    count = maps.shape[1]
    slab_index = lax.axis_index("rows")
    member = lax.axis_index("rep")
    pair_bit = member % 2
    field = maps[0] * mask.astype(jnp.float32)
    row_real, row_imag = row_transform(field)
    half_rows = extent // 2
    slabs = (
        row_real.reshape(count, extent // columns, columns),
        row_imag.reshape(count, extent // columns, columns),
    )
    spec_real, spec_imag = column_transform(
        (
            lax.all_to_all(slabs[0], "rows", split_axis=1, concat_axis=0, tiled=True),
            lax.all_to_all(slabs[1], "rows", split_axis=1, concat_axis=0, tiled=True),
        )
    )
    spec_real = spec_real.reshape(extent, columns)
    spec_imag = spec_imag.reshape(extent, columns)
    kept_real = lax.dynamic_slice_in_dim(spec_real, pair_bit * half_rows, half_rows, 0)
    kept_imag = lax.dynamic_slice_in_dim(spec_imag, pair_bit * half_rows, half_rows, 0)
    sent_real = lax.dynamic_slice_in_dim(spec_real, (1 - pair_bit) * half_rows, half_rows, 0)
    sent_imag = lax.dynamic_slice_in_dim(spec_imag, (1 - pair_bit) * half_rows, half_rows, 0)
    got_real, got_imag = partner((sent_real, sent_imag), "rep", 0)
    is_first = pair_bit == 0
    fields = (
        jnp.where(is_first, kept_real, got_real),
        jnp.where(is_first, kept_imag, got_imag),
        jnp.where(is_first, got_real, kept_real),
        jnp.where(is_first, got_imag, kept_imag),
    )
    own_bins = lax.dynamic_slice_in_dim(bins, pair_bit * half_rows, half_rows, 0)

    def frequency_of(offset, height):
        rows_here = lax.iota(jnp.int32, height)[:, None] + offset + pair_bit * half_rows
        cols_here = lax.iota(jnp.int32, columns)[None, :] + slab_index * columns
        return (rows_here, cols_here)

    block = min(256, half_rows)
    blocks = half_rows // block
    stacked = tuple((part.reshape(blocks, block, columns) for part in fields))
    bin_blocks = own_bins.reshape(blocks, block, columns)

    def accumulate(running, items):
        block_index, parts, bin_block = items
        rows_here, cols_here = frequency_of(block_index * block, block)
        term = band_terms(
            parts,
            signed_float(rows_here, extent),
            signed_float(cols_here, extent),
            bin_block,
            NBINS,
            extent,
        )
        return (running + term, None)

    partial_sums, _ = lax.scan(
        accumulate,
        jnp.zeros((3, NBINS), jnp.float32),
        (lax.iota(jnp.int32, blocks), stacked, bin_blocks),
    )
    sims_count = lax.axis_size("rep") // 2
    slot = (lax.iota(jnp.int32, sims_count) == member // 2).astype(jnp.float32)[:, None, None]
    totals = lax.psum(slot * partial_sums[None], ("rows", "rep"))
    auto = NBINS / (extent * extent)
    cross = math.sqrt(auto)
    factors = jnp.array([auto, auto, cross], jnp.float32)[None, :, None]
    return totals * factors


def solution(mesh):
    in_specs = (P("rep", "rows", None), P("rows", None), P(None, "rows"))
    out_specs = P()
    return jax.shard_map(
        on_device, mesh=mesh, in_specs=in_specs, out_specs=out_specs, check_vma=False
    )
```

profile of v0, /device:TPU:0, one launch (start us, length us, event | category | flops | bytes accessed | tf_op | source)
XLA Modules:
  0.0 1004.3 jit_solution(9013043201485757183)
XLA Ops:
  29.3 17.6 %fusion.37 = f32[64,512,64]{1,0,2:T(8,128)} fusion(f32[512,64,64]{0,2,1:T(8,128)} %bitcast.90), kind=kOutput, calls=%fused_computation.67 | convolution fusion | flops 1610674176 | bytes 16777216 | tf_op jit(solution)/shard_map/yan,ak->ykn/dot_general | solution.py:56
  46.9 21.0 %subtract_bitcast_fusion.1 = (f32[512,64,64]{0,1,2:T(8,128)S(1)}, f32[512,64,64]{0,1,2:T(8,128)}) fusion(f32[64,512,64]{1,0,2:T(8,128)} %fusion.37, f32[64,64]{0,1:T(8,128)S(1)} %get-tuple-element.245, f32[64,64]{0,1:T(8,128)S(1)} %get-tuple-element.246, f32[512,64,64]{0,2,1:T(8,128)} %bitcast.91), kind=kOutput, calls=%fused_computation.42 | convolution fusion | flops 1623252992 | bytes 33587200 | tf_op jit(solution)/shard_map/yan,ak->ykn/dot_general | solution.py:55
  67.9 19.2 %fusion.29 = f32[64,512,64]{1,0,2:T(8,128)S(1)} fusion(f32[512,64,64]{0,1,2:T(8,128)} %get-tuple-element.240), kind=kOutput, calls=%fused_computation.59 | convolution fusion | flops 1610670080 | bytes 16777216 | tf_op jit(solution)/shard_map/ykn,nm->ymk/dot_general | solution.py:33
  117.9 16.3 %fusion.31 = f32[64,512,64]{1,0,2:T(8,128)S(1)} fusion(f32[512,64,64]{0,1,2:T(8,128)} %get-tuple-element.240), kind=kOutput, calls=%fused_computation.61 | convolution fusion | flops 1610674176 | bytes 16777216 | tf_op jit(solution)/shard_map/ykn,nm->ymk/dot_general | solution.py:33
  134.2 17.1 %subtract_bitcast_fusion = f32[512,64,64]{0,1,2:T(8,128)S(1)} fusion(f32[64,512,64]{1,0,2:T(8,128)S(1)} %fusion.31, f32[512,64,64]{0,1,2:T(8,128)} %copy-done), kind=kOutput, calls=%fused_computation.40 | convolution fusion | flops 1612767232 | bytes 25165824 | tf_op jit(solution)/shard_map/ykn,nm->ymk/dot_general | solution.py:33
  159.4 53.0 %all-to-all-done.1 = f32[512,8,512]{0,2,1:T(8,128)} async-done(((f32[512,8,512]{0,2,1:T(8,128)}), f32[512,8,512]{0,2,1:T(8,128)}, u32[]{:S(2)}, u32[]{:S(2)}) %all-to-all-start.1) | async-done | bytes 8388640 | tf_op jit(solution)/shard_map/all_to_all | solution.py:136
  226.9 17.8 %fusion.21 = f32[64,64,512]{2,0,1:T(8,128)} fusion(f32[64,64,512]{2,1,0:T(8,128)} %bitcast.92), kind=kOutput, calls=%fused_computation.51 | convolution fusion | flops 1610670080 | bytes 16777216 | tf_op jit(solution)/shard_map/anbc,ak->knbc/dot_general | solution.py:33
  258.5 53.4 %all-to-all-done = f32[512,8,512]{0,2,1:T(8,128)} async-done(((f32[512,8,512]{0,2,1:T(8,128)}), f32[512,8,512]{0,2,1:T(8,128)}, u32[]{:S(2)}, u32[]{:S(2)}) %all-to-all-start) | async-done | bytes 8388640 | tf_op jit(solution)/shard_map/all_to_all | solution.py:135
  321.0 17.7 %fusion.27 = f32[64,64,512]{2,0,1:T(8,128)} fusion(f32[64,64,512]{2,1,0:T(8,128)} %bitcast.94), kind=kOutput, calls=%fused_computation.57 | convolution fusion | flops 1610670080 | bytes 16777216 | tf_op jit(solution)/shard_map/anbc,ak->knbc/dot_general | solution.py:33
  338.7 24.6 %multiply_subtract_fusion = (f32[64,64,512]{2,0,1:T(8,128)}, f32[64,64,512]{2,0,1:T(8,128)}) fusion(f32[64,64]{0,1:T(8,128)S(1)} %get-tuple-element.245, f32[64,64]{0,1:T(8,128)S(1)} %get-tuple-element.246, f32[64,64,512]{2,0,1:T(8,128)} %fusion.21, f32[64,64,512]{2,0,1:T(8,128)} %fusion.27, f32[64,64,512]{2,0,1:T(8,128)} %fusion.23, ...), kind=kOutput, calls=%fused_computation.38 | convolution fusion | flops 1627451392 | bytes 50364416 | tf_op jit(solution)/shard_map/anbc,ak->knbc/dot_general | solution.py:33
  363.3 18.5 %fusion.13 = f32[64,64,512]{2,0,1:T(8,128)} fusion(f32[64,64,512]{2,0,1:T(8,128)} %get-tuple-element.238), kind=kOutput, calls=%fused_computation.43 | convolution fusion | flops 1610670080 | bytes 16777216 | tf_op jit(solution)/shard_map/knbc,nm->mkbc/dot_general | solution.py:33
  394.3 15.6 %fusion.48 = f32[64,64,512]{2,0,1:T(8,128)} fusion(f32[64,64,512]{2,0,1:T(8,128)} %fusion.13, f32[64,64,512]{2,0,1:T(8,128)S(1)} %bitcast.89), kind=kOutput, calls=%fused_computation.76 | convolution fusion | flops 1612771328 | bytes 25165824 | tf_op jit(solution)/shard_map/knbc,nm->mkbc/dot_general | solution.py:33
  460.7 59.4 %collective-permute-done.1 = f32[2048,512]{1,0:T(8,128)} collective-permute-done((f32[2048,512]{1,0:T(8,128)}, f32[2048,512]{1,0:T(8,128)}, u32[]{:S(2)}, u32[]{:S(2)}) %collective-permute-start.1) | collective-permute-done | bytes 4194336 | tf_op jit(solution)/shard_map/ppermute | solution.py:15
  528.2 78.0 %collective-permute-done = f32[2048,512]{1,0:T(8,128)} collective-permute-done((f32[2048,512]{1,0:T(8,128)}, f32[2048,512]{1,0:T(8,128)}, u32[]{:S(2)}, u32[]{:S(2)}) %collective-permute-start) | collective-permute-done | bytes 4194336 | tf_op jit(solution)/shard_map/ppermute | solution.py:15
  612.8 348.4 %while.14 = (s32[]{:T(128)}, f32[3,1024]{1,0:T(4,128)S(1)}, s32[]{:T(128)}, s32[8]{0:T(128)S(1)}, s32[]{:T(128)}, /*index=5*/f32[8,256,512]{2,1,0:T(8,128)}, f32...) while((s32[]{:T(128)}, f32[3,1024]{1,0:T(4,128)S(1)}, ...), condition=%wide.region_1.2_spmd.clone, body=%wide.region_0.1_spmd.clone.sunk | while | flops 832713472 | bytes 68505800 | solution.py:178
  622.1 28.9 %copy.81 = bf16[6,8,256,512]{3,1,2,0:T(8,128)(2,1)S(1)} copy(bf16[6,8,256,512]{3,2,1,0:T(8,128)(2,1)S(1)} %bitcast.86) | data formatting | bytes 25165824 | tf_op jit(solution)/shard_map/while
  665.6 28.9 %copy.81 = bf16[6,8,256,512]{3,1,2,0:T(8,128)(2,1)S(1)} copy(bf16[6,8,256,512]{3,2,1,0:T(8,128)(2,1)S(1)} %bitcast.86) | data formatting | bytes 25165824 | tf_op jit(solution)/shard_map/while
  709.2 28.9 %copy.81 = bf16[6,8,256,512]{3,1,2,0:T(8,128)(2,1)S(1)} copy(bf16[6,8,256,512]{3,2,1,0:T(8,128)(2,1)S(1)} %bitcast.86) | data formatting | bytes 25165824 | tf_op jit(solution)/shard_map/while
  752.7 28.9 %copy.81 = bf16[6,8,256,512]{3,1,2,0:T(8,128)(2,1)S(1)} copy(bf16[6,8,256,512]{3,2,1,0:T(8,128)(2,1)S(1)} %bitcast.86) | data formatting | bytes 25165824 | tf_op jit(solution)/shard_map/while
  796.2 28.9 %copy.81 = bf16[6,8,256,512]{3,1,2,0:T(8,128)(2,1)S(1)} copy(bf16[6,8,256,512]{3,2,1,0:T(8,128)(2,1)S(1)} %bitcast.86) | data formatting | bytes 25165824 | tf_op jit(solution)/shard_map/while
  839.7 28.9 %copy.81 = bf16[6,8,256,512]{3,1,2,0:T(8,128)(2,1)S(1)} copy(bf16[6,8,256,512]{3,2,1,0:T(8,128)(2,1)S(1)} %bitcast.86) | data formatting | bytes 25165824 | tf_op jit(solution)/shard_map/while
  883.3 28.9 %copy.81 = bf16[6,8,256,512]{3,1,2,0:T(8,128)(2,1)S(1)} copy(bf16[6,8,256,512]{3,2,1,0:T(8,128)(2,1)S(1)} %bitcast.86) | data formatting | bytes 25165824 | tf_op jit(solution)/shard_map/while
  926.8 28.9 %copy.81 = bf16[6,8,256,512]{3,1,2,0:T(8,128)(2,1)S(1)} copy(bf16[6,8,256,512]{3,2,1,0:T(8,128)(2,1)S(1)} %bitcast.86) | data formatting | bytes 25165824 | tf_op jit(solution)/shard_map/while
  961.3 41.8 %psum.7 = f32[2,3,1024]{2,0,1:T(2,128)S(1)} all-reduce(f32[2,3,1024]{2,0,1:T(2,128)S(1)} %broadcast_multiply_fusion.2), channel_id=1, replica_groups=mesh['rows'=8,'rep'=4] {'rows','rep'}, use_global_device_ids=true, to_apply=%region_2.3 | all-reduce | flops 6144 | bytes 49152 | tf_op jit(solution)/shard_map/psum | solution.py:185
  (160 shorter events, 295.2 us)
Async XLA Ops:
  67.9 19.2 %copy-start = (f32[512,64,64]{0,1,2:T(8,128)}, f32[512,64,64]{0,1,2:T(8,128)S(1)}, u32[]{:S(2)}) copy-start(f32[512,64,64]{0,1,2:T(8,128)S(1)} %get-tuple-element.239) | copy-start | bytes 25165828
  112.5 100.0 %all-to-all-start.1 = ((f32[512,8,512]{0,2,1:T(8,128)}), f32[512,8,512]{0,2,1:T(8,128)}, u32[]{:S(2)}, u32[]{:S(2)}) async-start(f32[512,8,512]{0,2,1:T(8,128)} %bitcast.103), calls=%async_computation.1 | async-start | bytes 16777216 | tf_op jit(solution)/shard_map/all_to_all | solution.py:136
  212.4 99.4 %all-to-all-start = ((f32[512,8,512]{0,2,1:T(8,128)}), f32[512,8,512]{0,2,1:T(8,128)}, u32[]{:S(2)}, u32[]{:S(2)}) async-start(f32[512,8,512]{0,2,1:T(8,128)} %bitcast.102), calls=%async_computation | async-start | bytes 16777216 | tf_op jit(solution)/shard_map/all_to_all | solution.py:135
  226.9 17.8 %copy-start.1 = (f32[8,512,1,512]{3,1,0,2:T(8,128)S(1)}, f32[8,512,1,512]{3,1,0,2:T(8,128)}, u32[]{:S(2)}) copy-start(f32[8,512,1,512]{3,1,0,2:T(8,128)} %copy.27) | copy-start | bytes 25165828
  363.3 18.5 %copy-start.2 = (f32[64,64,512]{2,0,1:T(8,128)S(1)}, f32[64,64,512]{2,0,1:T(8,128)}, u32[]{:S(2)}) copy-start(f32[64,64,512]{2,0,1:T(8,128)} %get-tuple-element.238) | copy-start | bytes 25165828
  363.3 31.0 %slice-start = ((s8[8388608]{0:T(1024)(128)(4,1)}), s8[4194304]{0:T(1024)(128)(4,1)S(1)}, s32[]{:S(2)}) async-start(s8[8388608]{0:T(1024)(128)(4,1)} %bitcast.88), calls=%async_computation.2 | async-start | bytes 8388608
  381.8 12.5 %slice-start.1 = ((s8[8388608]{0:T(1024)(128)(4,1)}), s8[4194304]{0:T(1024)(128)(4,1)S(1)}, s32[]{:S(2)}) async-start(s8[8388608]{0:T(1024)(128)(4,1)} %bitcast.88), calls=%async_computation.3 | async-start | bytes 8388608
  426.1 94.0 %collective-permute-start.1 = (f32[2048,512]{1,0:T(8,128)}, f32[2048,512]{1,0:T(8,128)}, u32[]{:S(2)}, u32[]{:S(2)}) collective-permute-start(f32[2048,512]{1,0:T(8,128)} %constant_dynamic-slice_fusion.1), channel_id=1, source_target_pairs={{0,1},{1,0},{2,3},{3,2},{4,5},{5,4},{6,7},{7,6},{8,9},{9,8},{10,11... | collective-permute-start | bytes 12582920 | tf_op jit(solution)/shard_map/ppermute | solution.py:15
  450.2 3.2 copy-start.3
  455.9 150.3 %collective-permute-start = (f32[2048,512]{1,0:T(8,128)}, f32[2048,512]{1,0:T(8,128)}, u32[]{:S(2)}, u32[]{:S(2)}) collective-permute-start(f32[2048,512]{1,0:T(8,128)} %constant_dynamic-slice_fusion.2), channel_id=1, source_target_pairs={{0,1},{1,0},{2,3},{3,2},{4,5},{5,4},{6,7},{7,6},{8,9},{9,8},{10,11... | collective-permute-start | bytes 12582920 | tf_op jit(solution)/shard_map/ppermute | solution.py:15
  455.9 150.3 %slice-start.2 = ((s8[8388608]{0:T(1024)(128)(4,1)}), s8[4194304]{0:T(1024)(128)(4,1)S(1)}, s32[]{:S(2)}) async-start(s8[8388608]{0:T(1024)(128)(4,1)} %bitcast.99), calls=%async_computation.4 | async-start | bytes 8388608
  460.7 145.5 %slice-start.3 = ((s8[8388608]{0:T(1024)(128)(4,1)}), s8[4194304]{0:T(1024)(128)(4,1)S(1)}, s32[]{:S(2)}) async-start(s8[8388608]{0:T(1024)(128)(4,1)} %bitcast.99), calls=%async_computation.5 | async-start | bytes 8388608
  612.8 390.4 %copy-start.4 = (f32[3]{0:T(128)S(1)}, f32[3]{0:T(128)}, u32[]{:S(2)}) copy-start(f32[3]{0:T(128)} %constant.195.clone) | copy-start | bytes 40
where the time goes:
time: 1010 us; the launch traced here: 1000 us
  local copies, waits for them, and re-layouts  329 us (33%)
  matrix products  282 us (28%)
  waiting for transfers between devices  244 us (24%)
  other arithmetic  87.5 us (9%)
  blocking collectives  41.8 us (4%)
  starting transfers between devices  13.1 us (1%)
    while x16, local copies, waits for them, and re-layouts  233 us
    dot_general x12, matrix products, product(): return jnp.einsum(form, left, right, precision=precise)  201 us
    ppermute x2, waiting for transfers between devices, partner(): lax.ppermute(array, axis, [(i, i ^ 1 << distance) for i in range(lax.axis...  137 us
    all_to_all x1, waiting for transfers between devices, on_device(): lax.all_to_all(slabs[0], 'rows', split_axis=1, concat_axis=0, tiled=True)  53.4 us
    all_to_all x1, waiting for transfers between devices, on_device(): lax.all_to_all(slabs[1], 'rows', split_axis=1, concat_axis=0, tiled=True)  53 us
    dot_general x8, matrix products, band_terms(): lax.dot_general(weighted, low_hot, (((1,), (1,)), ((), ())), preferred_el...  43.1 us
    psum x1, blocking collectives, on_device(): totals = lax.psum(slot * partial_sums[None], ('rows', 'rep'))  41.8 us
    add x2, local copies, waits for them, and re-layouts, complex_apply(): product(real_part, table_sin) + product(imag_part, table_cos)  23 us
  transfers between devices with their start and end apart: 4, of which 4 were waited for; matrix products, arithmetic and copies ran while one was open for 12% of the time, Pallas kernels for 0%

commit v1 on v0

--- a/solution.py
+++ b/solution.py
@@ -1,8 +1,12 @@
+import functools
 import math
 
 import jax
 import jax.numpy as jnp
+import numpy as np
 from jax import lax
+from jax.experimental import pallas as pl
+from jax.experimental.pallas import tpu as pltpu
 from jax.sharding import PartitionSpec as P
 
 NBINS = 1024
@@ -189,9 +193,473 @@
     return totals * factors
 
 
+LANES = 128
+OUTER = 32
+HALF = LANES // 2
+GROUPS = 16
+LOWS = 64
+
+
+def fft_wave(index, size):
+    return (math.cos(2 * math.pi * index / size), -math.sin(2 * math.pi * index / size))
+
+
+def turned(value, index, size):
+    real, imag = value
+    if index == 0:
+        return value
+    if 4 * index == size:
+        return (imag, -real)
+    cosine, sine = fft_wave(index, size)
+    if 8 * index == size:
+        return ((real + imag) * cosine, (imag - real) * cosine)
+    if 8 * index == 3 * size:
+        return ((imag - real) * -cosine, (real + imag) * cosine)
+    return (real * cosine - imag * sine, real * sine + imag * cosine)
+
+
+def real_fft(values):
+    size = len(values)
+    if size == 2:
+        return [(values[0] + values[1], None), (values[0] - values[1], None)]
+    even = real_fft(values[0::2])
+    odd = real_fft(values[1::2])
+    half = size // 2
+    out = [None] * (half + 1)
+    out[0] = (even[0][0] + odd[0][0], None)
+    out[half] = (even[0][0] - odd[0][0], None)
+    quarter = size // 4
+    out[quarter] = (even[quarter][0], -odd[quarter][0])
+    for k in range(1, quarter):
+        real, imag = turned(odd[k], k, size)
+        out[k] = (even[k][0] + real, even[k][1] + imag)
+        out[half - k] = (even[k][0] - real, imag - even[k][1])
+    return out
+
+
+def complex_fft(values):
+    size = len(values)
+    if size == 1:
+        return values
+    even = complex_fft(values[0::2])
+    odd = complex_fft(values[1::2])
+    half = size // 2
+    out = [None] * size
+    for k in range(half):
+        real, imag = turned(odd[k], k, size)
+        out[k] = (even[k][0] + real, even[k][1] + imag)
+        out[k + half] = (even[k][0] - real, even[k][1] - imag)
+    return out
+
+
+def wave_matrix(angles):
+    cosine, sine = np.cos(angles), np.sin(angles)
+    return cosine, sine
+
+
+def host_tables(extent):
+    b = np.arange(LANES)[:, None]
+    k = np.arange(LANES)[None, :]
+    cosine, sine = wave_matrix(2 * np.pi * (b * k % LANES) / LANES)
+    top = np.concatenate([cosine, -sine], 1)
+    low = np.concatenate([sine, cosine], 1)
+    natural = np.concatenate([top, low], 0)
+    order = np.concatenate(
+        [np.arange(HALF), LANES + np.arange(HALF), HALF + np.arange(HALF), LANES + HALF + np.arange(HALF)]
+    )
+    family = natural[:, order]
+    first = np.zeros((2 * LANES, 2 * LANES))
+    i = np.arange(HALF)[None, :]
+    cosine, sine = wave_matrix(2 * np.pi * (b * i % LANES) / LANES)
+    first[:LANES, :HALF] = cosine
+    first[:LANES, HALF:LANES] = -sine
+    first[:LANES, HALF] = 1.0 - 2.0 * (np.arange(LANES) % 2)
+    freq = OUTER // 2 + OUTER * (HALF - 1 - i)
+    cosine, sine = wave_matrix(2 * np.pi * (b * freq % extent) / extent)
+    first[LANES:, LANES : LANES + HALF] = cosine
+    first[LANES:, LANES + HALF :] = -sine
+    return first, family, natural
+
+
+def split_table(table):
+    table = jnp.asarray(table, jnp.float32)
+    high = table.astype(jnp.bfloat16)
+    return high, (table - high.astype(jnp.float32)).astype(jnp.bfloat16)
+
+
+def split_value(value):
+    high = value.astype(jnp.bfloat16)
+    return high, (value - high.astype(jnp.float32)).astype(jnp.bfloat16)
+
+
+def dot_f32(left, right, dims=(((1,), (0,)), ((), ()))):
+    return lax.dot_general(left, right, dims, preferred_element_type=jnp.float32)
+
+
+def three_pass(value, table_high, table_low):
+    high, low = split_value(value)
+    return dot_f32(high, table_high) + (dot_f32(low, table_high) + dot_f32(high, table_low))
+
+
+def row_kernel(map_ref, mask_ref, turn_ref, high_ref, low_ref, out0_ref, out1_ref, mid_ref):
+    block = map_ref.shape[1]
+
+    def tile(step, carry):
+        start = pl.multiple_of(step * 8, 8)
+        cells = []
+        for a in range(OUTER):
+            lanes = pl.ds(a * LANES, LANES)
+            weight = mask_ref[pl.ds(start, 8), lanes].astype(jnp.float32)
+            cells.append(map_ref[0, pl.ds(start, 8), lanes] * weight)
+        waves = real_fft(cells)
+        half = OUTER // 2
+        mid_ref[0, pl.ds(start, 8), 0:LANES] = waves[0][0]
+        mid_ref[0, pl.ds(start, 8), LANES : 2 * LANES] = waves[half][0]
+        for k in range(1, half):
+            real, imag = waves[k]
+            cosine = turn_ref[0, k : k + 1, :]
+            sine = turn_ref[1, k : k + 1, :]
+            mid_ref[k, pl.ds(start, 8), 0:LANES] = real * cosine - imag * sine
+            mid_ref[k, pl.ds(start, 8), LANES : 2 * LANES] = real * sine + imag * cosine
+        return carry
+
+    lax.fori_loop(0, block // 8, tile, 0)
+
+    def family(k, carry):
+        which = jnp.minimum(k, 1)
+        value = three_pass(mid_ref[k], high_ref[which], low_ref[which])
+        out0_ref[k] = value[:, :LANES]
+        out1_ref[k] = value[:, LANES:]
+        return carry
+
+    lax.fori_loop(0, OUTER // 2, family, 0)
+
+
+def bins_kernel(info_ref, bins_ref, flip_ref, out_ref, both_ref):
+    step = pl.program_id(0)
+    sub = bins_ref.shape[1]
+    parity = info_ref[0]
+    upper = info_ref[1]
+    dests = out_ref.shape[0]
+    width = out_ref.shape[3]
+    for c in range(sub):
+        kappa = step * sub + c
+        mirrored = (OUTER - kappa) % OUTER
+        turned_bins = bins_ref[:, c, :].astype(jnp.float32).T
+        high = jnp.floor(turned_bins * 0.125)
+        low = turned_bins - high * 8.0
+        pair = jnp.concatenate([high.astype(jnp.bfloat16), low.astype(jnp.bfloat16)], 1)
+        both_ref[0] = turned_bins
+        both_ref[1] = dot_f32(pair, flip_ref[jnp.minimum(kappa, 1)])
+        for dest in range(dests):
+            fam = 2 * dest + parity
+            zero = fam == 0
+            col0 = jnp.where(zero & (upper == 1), OUTER // 2, fam)
+            rev0 = jnp.where(zero & (upper == 1), 1, 0)
+            col1 = jnp.where(zero, jnp.where(upper == 1, 0, OUTER // 2), OUTER - fam)
+            rev1 = jnp.where(zero & (upper == 0), 0, 1)
+            k0 = jnp.where(rev0 == 1, mirrored, kappa)
+            k1 = jnp.where(rev1 == 1, mirrored, kappa)
+            out_ref[dest, 0, k0] = both_ref[rev0, pl.ds(col0, width, stride=OUTER), :]
+            out_ref[dest, 1, k1] = both_ref[rev1, pl.ds(col1, width, stride=OUTER), :]
+
+
+def band_kernel(
+    extent, nbins, chunk, info_ref, x_ref, bins0_ref, bins1_ref, turn_ref, high_ref, low_ref, fx_ref,
+    sums_ref, edge_ref, mid_ref, power_ref, part_ref,
+):
+    offset = info_ref[0]
+    flipped = info_ref[1]
+    hollow = info_ref[2]
+    local = x_ref.shape[2]
+    per_slab = local // LANES
+    lane8 = lax.broadcasted_iota(jnp.int32, (8, LANES), 1)
+    left8 = lane8 < HALF
+
+    def tile(step, carry):
+        start = pl.multiple_of(step * 8, 8)
+        cells = []
+        for a in range(OUTER):
+            rows = pl.ds((a % per_slab) * LANES + start, 8)
+            q = x_ref[a // per_slab, 0, rows, :]
+            u = x_ref[a // per_slab, 1, rows, :]
+            real = jnp.where(left8, q, pltpu.roll(u, HALF, 1))
+            imag = jnp.where(left8, pltpu.roll(q, HALF, 1), u)
+            cells.append((real, imag))
+        waves = complex_fft(cells)
+        turns = {1: (turn_ref[0, pl.ds(start, 8), :], turn_ref[1, pl.ds(start, 8), :])}
+        mid_ref[0, pl.ds(start, 8), :] = waves[0][0]
+        mid_ref[0, pl.ds(LANES + start, 8), :] = waves[0][1]
+        for k in range(1, OUTER):
+            if k not in turns:
+                (ar, ai), (br, bi) = turns[k // 2], turns[k - k // 2]
+                turns[k] = (ar * br - ai * bi, ar * bi + ai * br)
+            cosine, sine = turns[k]
+            real, imag = waves[k]
+            mid_ref[k, pl.ds(start, 8), :] = real * cosine - imag * sine
+            mid_ref[k, pl.ds(LANES + start, 8), :] = real * sine + imag * cosine
+        return carry
+
+    lax.fori_loop(0, LANES // 8, tile, 0)
+
+    fx = fx_ref[...]
+    lane = lax.broadcasted_iota(jnp.int32, (HALF, LANES), 1)
+    slot = lax.broadcasted_iota(jnp.int32, (HALF, LANES), 0)
+    keep = jnp.where((slot == 0) & (hollow == 1), 0.0, 1.0)
+    inv_area = 1.0 / (extent * extent)
+    group_iota = lax.broadcasted_iota(jnp.int32, (GROUPS, LANES), 0).astype(jnp.float32).astype(jnp.bfloat16)
+    low_iota = lax.broadcasted_iota(jnp.int32, (LOWS, LANES), 0).astype(jnp.float32).astype(jnp.bfloat16)
+    width = bins0_ref.shape[3]
+    one = jnp.ones((LOWS, LANES), jnp.bfloat16)
+    none = jnp.zeros((LOWS, LANES), jnp.bfloat16)
+    empty = jnp.zeros((GROUPS, LANES), jnp.bfloat16)
+    unroll = 8
+
+    def family(k, acc):
+        spectrum = three_pass(mid_ref[k].T, high_ref[...], low_ref[...])
+        if chunk == 0:
+            edge_ref[k, 0:1, :] = spectrum[0:1, :]
+            edge_ref[k, 1:2, :] = spectrum[HALF : HALF + 1, :]
+        q_real, q_imag = spectrum[:HALF, :LANES], spectrum[:HALF, LANES:]
+        u_real, u_imag = spectrum[HALF:, :LANES], spectrum[HALF:, LANES:]
+        row = lane * OUTER + k
+        fy = jnp.where(row >= extent // 2, row - extent, row).astype(jnp.float32)
+        radius = jnp.maximum(fx * fx + fy * fy, 1.0)
+        cos_twice = (fx * fx - fy * fy) / radius
+        sin_twice = 2.0 * fx * fy / radius
+
+        def powers(sine, which):
+            e_real = cos_twice * q_real + sine * u_real
+            e_imag = cos_twice * q_imag + sine * u_imag
+            b_real = cos_twice * u_real - sine * q_real
+            b_imag = cos_twice * u_imag - sine * q_imag
+            power_ref[which, 0] = (e_real * e_real + e_imag * e_imag) * inv_area * keep
+            power_ref[which, 1] = (b_real * b_real + b_imag * b_imag) * inv_area * keep
+            power_ref[which, 2] = (e_real * b_real + e_imag * b_imag) * inv_area * keep
+
+        other = jnp.where(k == 0, 1, 0)
+        powers(sin_twice, jnp.where(k == 0, 1 - flipped, 0))
+
+        @pl.when(k == 0)
+        def _():
+            powers(jnp.where(row == extent // 2, -sin_twice, sin_twice), flipped)
+
+        for index, bins_ref in enumerate((bins0_ref, bins1_ref)):
+            for source in range(bins_ref.shape[0]):
+                value = bins_ref[source, 0, k]
+                high = jnp.floor(value * (1.0 / LOWS))
+                part_ref[index, 0, source * width : (source + 1) * width] = high
+                part_ref[index, 1, source * width : (source + 1) * width] = value - high * LOWS
+
+        def slots(step, acc):
+            weighted, lows = [], []
+            for inner in range(unroll):
+                i = step * unroll + inner
+                mirror = (offset - i) & (HALF - 1)
+                for index, at, source in ((0, i, 0), (1, mirror, other)):
+                    def line(ref, *where_):
+                        return ref[where_ + (pl.ds(at, 1), slice(None))]
+                    high = part_ref[index, 0, pl.ds(at, 1), :]
+                    low = part_ref[index, 1, pl.ds(at, 1), :]
+                    high = jnp.broadcast_to(high, (GROUPS, LANES)).astype(jnp.bfloat16)
+                    low = jnp.broadcast_to(low, (LOWS, LANES)).astype(jnp.bfloat16)
+                    hot = high == group_iota
+                    column = []
+                    for kind in range(3):
+                        power = power_ref[source, kind, pl.ds(i, 1), :]
+                        power = jnp.broadcast_to(power, (GROUPS, LANES)).astype(jnp.bfloat16)
+                        column.append(jnp.where(hot, power, empty))
+                    weighted.append(jnp.concatenate(column, 0))
+                    lows.append(jnp.where(low == low_iota, one, none))
+            return acc + dot_f32(
+                jnp.concatenate(weighted, 1), jnp.concatenate(lows, 1), (((1,), (1,)), ((), ()))
+            )
+
+        return lax.fori_loop(0, HALF // unroll, slots, acc)
+
+    sums_ref[...] = lax.fori_loop(0, OUTER, family, jnp.zeros((3 * GROUPS, LOWS), jnp.float32))
+
+
+def vmem_spec(*block):
+    if block:
+        return pl.BlockSpec(*block)
+    return pl.BlockSpec(memory_space=pltpu.VMEM)
+
+
+def summed(array, axis):
+    distance = 0
+    while 1 << distance < lax.axis_size(axis):
+        array = array + partner(array, axis, distance)
+        distance += 1
+    return array
+
+
+def edge_sums(edge, bins_left, bins_right, extent):
+    flat = edge.transpose(1, 2, 0).reshape(2, 2, extent)
+    back = jnp.roll(flat[:, :, ::-1], 1, axis=2)
+    q_real, q_imag, u_real, u_imag = [
+        jnp.stack(pair)
+        for m in range(2)
+        for pair in (
+            (0.5 * (flat[m, 0] + back[m, 0]), 0.5 * (flat[m, 1] + back[m, 1])),
+            (0.5 * (flat[m, 1] - back[m, 1]), 0.5 * (back[m, 0] - flat[m, 0])),
+        )
+    ]
+    freq_y = signed_float(lax.iota(jnp.int32, extent), extent)[None, :]
+    freq_x = jnp.array([0.0, -extent // 2], jnp.float32)[:, None]
+    left = bins_left.T.reshape(extent)
+    right = jnp.roll(bins_right.T.reshape(extent)[::-1], 1)
+    bins = jnp.stack([left, right]).astype(jnp.int32)
+    return band_terms((q_real, q_imag, u_real, u_imag), freq_y, freq_x, bins, NBINS, extent)
+
+
+def on_device_fast(maps, mask, bins):
+    extent = bins.shape[0]
+    columns = bins.shape[1]
+    count = maps.shape[1]
+    slabs = lax.axis_size("rows")
+    reps = lax.axis_size("rep")
+    slab_index = lax.axis_index("rows")
+    member = lax.axis_index("rep")
+    pair_bit = member % 2
+    half_slabs = slabs // 2
+    first, family, natural = host_tables(extent)
+    row_high, row_low = split_table(np.stack([first, family]))
+    col_high, col_low = split_table(natural)
+
+    flips = np.zeros((2, 2 * LANES, LANES))
+    for k in range(LANES):
+        flips[0, k, -k % LANES] = 8.0
+        flips[0, LANES + k, -k % LANES] = 1.0
+        flips[1, k, LANES - 1 - k] = 8.0
+        flips[1, LANES + k, LANES - 1 - k] = 1.0
+    info = jnp.stack([pair_bit, (slab_index >= half_slabs).astype(jnp.int32)])
+    sub = 8
+    width = columns // OUTER
+    sent_bins = pl.pallas_call(
+        bins_kernel,
+        grid=(OUTER // sub,),
+        in_specs=[
+            pl.BlockSpec(memory_space=pltpu.SMEM),
+            pl.BlockSpec((LANES, sub, columns), lambda i: (0, i, 0)),
+            pl.BlockSpec((2, 2 * LANES, LANES), lambda i: (0, 0, 0)),
+        ],
+        out_specs=pl.BlockSpec((slabs, 2, OUTER, width, LANES), lambda i: (0, 0, 0, 0, 0)),
+        out_shape=jax.ShapeDtypeStruct((slabs, 2, OUTER, width, LANES), jnp.float32),
+        scratch_shapes=[pltpu.VMEM((2, columns, LANES), jnp.float32)],
+        name="bins_prep",
+    )(info, bins.reshape(LANES, OUTER, columns), jnp.asarray(flips, jnp.bfloat16))
+    got_bins = lax.all_to_all(sent_bins, "rows", split_axis=0, concat_axis=0, tiled=True)
+
+    block = min(LANES, count)
+    k1 = np.arange(OUTER // 2)[:, None]
+    angles = 2 * np.pi * (k1 * np.arange(LANES)[None, :] % extent) / extent
+    turns = jnp.asarray(np.stack([np.cos(angles), -np.sin(angles)]), jnp.float32)
+    table_spec = pl.BlockSpec((2, 2 * LANES, 2 * LANES), lambda i: (0, 0, 0))
+    piece = jax.ShapeDtypeStruct((2 * slabs, count, LANES), jnp.float32)
+    piece_spec = pl.BlockSpec((2 * slabs, block, LANES), lambda i: (0, i, 0))
+    pieces = pl.pallas_call(
+        row_kernel,
+        grid=(count // block,),
+        in_specs=[
+            pl.BlockSpec((1, block, extent), lambda i: (0, i, 0)),
+            pl.BlockSpec((block, extent), lambda i: (i, 0)),
+            pl.BlockSpec(turns.shape, lambda i: (0, 0, 0)),
+            table_spec,
+            table_spec,
+        ],
+        out_specs=[piece_spec, piece_spec],
+        out_shape=[piece, piece],
+        scratch_shapes=[pltpu.VMEM((OUTER // 2, block, 2 * LANES), jnp.float32)],
+        name="row_fft",
+    )(maps, mask, turns, row_high, row_low)
+
+    groups = [
+        [row * reps + z for row in range(slabs) for z in (2 * sky, 2 * sky + 1)]
+        for sky in range(reps // 2)
+    ]
+    fam = 2 * slab_index + pair_bit
+    angles = 2 * np.pi * np.arange(LANES) / extent
+    spin = np.stack([np.cos(angles), -np.sin(angles)])[:, :, None]
+    spin = jnp.asarray(np.broadcast_to(spin, (2, LANES, LANES)), jnp.float32)
+    slots = lax.iota(jnp.int32, HALF)
+    total = None
+    for chunk in range(2):
+        got = lax.all_to_all(
+            pieces[chunk], ("rows", "rep"), split_axis=0, concat_axis=0, tiled=True,
+            axis_index_groups=groups,
+        ).reshape(slabs, 2, count, LANES)
+        first_col = OUTER * slots if chunk == 0 else OUTER // 2 + OUTER * (HALF - 1 - slots)
+        col = jnp.where(fam == 0, first_col, fam + OUTER * (slots + HALF * chunk))
+        fx = jnp.broadcast_to(signed_float(col, extent)[:, None], (HALF, LANES))
+        zero = (fam == 0).astype(jnp.int32)
+        if chunk == 0:
+            info = jnp.stack([HALF - 1 + zero, jnp.int32(1), zero])
+        else:
+            info = jnp.stack([jnp.int32(HALF - 1), 1 - zero, jnp.int32(0)])
+        bin_block = (half_slabs, 1, OUTER, width, LANES)
+        sums, edge = pl.pallas_call(
+            functools.partial(band_kernel, extent, NBINS, chunk),
+            grid=(1,),
+            in_specs=[
+                pl.BlockSpec(memory_space=pltpu.SMEM),
+                pl.BlockSpec(got.shape, lambda i: (0, 0, 0, 0)),
+                pl.BlockSpec(bin_block, lambda i, at=chunk: (at, 0, 0, 0, 0)),
+                pl.BlockSpec(bin_block, lambda i, at=1 - chunk: (at, 1, 0, 0, 0)),
+                pl.BlockSpec(spin.shape, lambda i: (0, 0, 0)),
+                pl.BlockSpec(col_high.shape, lambda i: (0, 0)),
+                pl.BlockSpec(col_low.shape, lambda i: (0, 0)),
+                pl.BlockSpec(fx.shape, lambda i: (0, 0)),
+            ],
+            out_specs=[
+                pl.BlockSpec((3 * GROUPS, LOWS), lambda i: (0, 0)),
+                pl.BlockSpec((OUTER, 2, 2 * LANES), lambda i: (0, 0, 0)),
+            ],
+            out_shape=[
+                jax.ShapeDtypeStruct((3 * GROUPS, LOWS), jnp.float32),
+                jax.ShapeDtypeStruct((OUTER, 2, 2 * LANES), jnp.float32),
+            ],
+            scratch_shapes=[
+                pltpu.VMEM((OUTER, 2 * LANES, LANES), jnp.float32),
+                pltpu.VMEM((2, 3, HALF, LANES), jnp.float32),
+                pltpu.VMEM((2, 2, HALF, LANES), jnp.float32),
+            ],
+            compiler_params=pltpu.CompilerParams(vmem_limit_bytes=48 * 2**20),
+            name="band_sums",
+        )(info, got, got_bins, got_bins, spin, col_high, col_low, fx)
+        total = sums if total is None else total + sums
+        if chunk == 0:
+            special = edge_sums(edge, got_bins[0, 0, :, 0], got_bins[half_slabs, 1, :, 0], extent)
+            special = jnp.where(fam == 0, special, 0.0)
+    partial_sums = total.reshape(3, NBINS) + special
+    auto = NBINS / (extent * extent)
+    cross = math.sqrt(auto)
+    factors = jnp.array([auto, auto, cross], jnp.float32)[:, None]
+    own = summed(partial_sums, "rows")
+    own = (own + partner(own, "rep", 0)) * factors
+    skies = [own]
+    distance = 1
+    while 1 << distance < reps:
+        skies = skies + [partner(sky, "rep", distance) for sky in skies]
+        distance += 1
+    stacked = jnp.stack(skies)
+    order = lax.iota(jnp.int32, len(skies)) ^ (member // 2)
+    return jnp.take(stacked, order, axis=0) if len(skies) > 2 else jnp.where(
+        member // 2 == 0, stacked, stacked[::-1]
+    )
+
+
 def solution(mesh):
     in_specs = (P("rep", "rows", None), P("rows", None), P(None, "rows"))
     out_specs = P()
+
+    def on_any(maps, mask, bins):
+        extent = bins.shape[0]
+        families = 2 * lax.axis_size("rows")
+        if extent == OUTER * LANES and families == OUTER // 2 and NBINS == GROUPS * LOWS:
+            return on_device_fast(maps, mask, bins)
+        return on_device(maps, mask, bins)
+
     return jax.shard_map(
-        on_device, mesh=mesh, in_specs=in_specs, out_specs=out_specs, check_vma=False
-    )
+        on_any, mesh=mesh, in_specs=in_specs, out_specs=out_specs, check_vma=False
+    )

time: 1010 us -> 305 us (0.30)
  local copies, waits for them, and re-layouts: 329 us -> 6.96 us
  matrix products: 282 us -> 0.47 us
  Pallas kernels: 0 us -> 179 us
  waiting for transfers between devices: 244 us -> 88 us
  other arithmetic: 87.5 us -> 3.5 us
  blocking collectives: 41.8 us -> 0 us
  starting transfers between devices: 13.1 us -> 26 us
    dot_general x14 -> x0, matrix products: 239 us -> none  [the longest x12 201 us: product(): return jnp.einsum(form, left, right, precision=precise)]
    while x16 -> x0, local copies, waits for them, and re-layouts: 233 us -> none
    pallas_call x0 -> x4, Pallas kernels: none -> 179 us  [the longest x2 145 us: on_device_fast(): pl.pallas_call(functools.partial(band_kernel, extent, NBINS, chunk), grid...]
    ppermute x2 -> x5, waiting for transfers between devices: 137 us -> 8.18 us  [partner(): lax.ppermute(array, axis, [(i, i ^ 1 << distance) for i in range(lax.axis...]
    dot_general x8 -> x1, matrix products: 43.1 us -> 0.47 us  [band_terms(): lax.dot_general(weighted, low_hot, (((1,), (1,)), ((), ())), preferred_el...]
    psum x1 -> x0, blocking collectives: 41.8 us -> none  [on_device(): totals = lax.psum(slot * partial_sums[None], ('rows', 'rep'))]
    all_to_all x2 -> x3, waiting for transfers between devices: 106 us -> 79.8 us  [the longest x2 52.1 us: on_device_fast(): lax.all_to_all(pieces[chunk], ('rows', 'rep'), split_axis=0, concat_axis=...]
    add x2 -> x1, local copies, waits for them, and re-layouts: 23 us -> 0.08 us  [on_device_fast(): partial_sums = total.reshape(3, NBINS) + special]
  transfers between devices with their start and end apart: 4 -> 8, of which waited for: 4 -> 7; matrix products, arithmetic and copies ran while one was open for 12% -> 3% of each run, Pallas kernels for 0% -> 31%
where the time goes in v1:
time: 305 us
  Pallas kernels  179 us (59%)
  waiting for transfers between devices  88 us (29%)
  starting transfers between devices  26 us (9%)
  local copies, waits for them, and re-layouts  6.96 us (2%)
  other arithmetic  3.5 us (1%)
    pallas_call x2, Pallas kernels, on_device_fast(): pl.pallas_call(functools.partial(band_kernel, extent, NBINS, chunk), grid...  145 us
    all_to_all x2, waiting for transfers between devices, on_device_fast(): lax.all_to_all(pieces[chunk], ('rows', 'rep'), split_axis=0, concat_axis=...  52.1 us
    all_to_all x1, waiting for transfers between devices, on_device_fast(): lax.all_to_all(sent_bins, 'rows', split_axis=0, concat_axis=0, tiled=True)  27.8 us
    pallas_call x1, Pallas kernels, on_device_fast(): pl.pallas_call(row_kernel, grid=(count // block,), in_specs=[pl.BlockSpec...  21.4 us
    pallas_call x1, Pallas kernels, on_device_fast(): pl.pallas_call(bins_kernel, grid=(OUTER // sub,), in_specs=[pl.BlockSpec(...  13.3 us
    all_to_all x2, starting transfers between devices, on_device_fast(): lax.all_to_all(pieces[chunk], ('rows', 'rep'), split_axis=0, concat_axis=...  11.5 us
    ppermute x5, starting transfers between devices, partner(): lax.ppermute(array, axis, [(i, i ^ 1 << distance) for i in range(lax.axis...  9.36 us
    ppermute x5, waiting for transfers between devices, partner(): lax.ppermute(array, axis, [(i, i ^ 1 << distance) for i in range(lax.axis...  8.18 us
  transfers between devices with their start and end apart: 8, of which 7 were waited for; matrix products, arithmetic and copies ran while one was open for 3% of the time, Pallas kernels for 31%

profile of v1, /device:TPU:0, one launch (start us, length us, event | category | flops | bytes accessed | tf_op | source)
XLA Modules:
  0.0 304.8 jit_solution(14973212487120160117)
XLA Ops:
  0.0 0.6 pad_add_fusion.1.info_ref
  0.6 13.3 %bins_prep.1 = f32[8,2,32,16,128]{4,3,2,1,0:T(8,128)} custom-call(s32[2]{0:T(128)} %pad_add_fusion.1.info_ref, s32[128,32,512]{2,1,0:T(8,128)} %bitcast.29, bf16[2,256,128]{2,1,0:T(8,128)(2,1)} %constant.110.clone.flip_ref), custom_call_target="tpu_custom_call" | custom-call | tf_op jit(solution)/shard_map/bins_prep/pallas_call | solution.py:539
  13.9 5.2 %all-to-all-start.1 = ((f32[8,2,32,16,128]{4,3,2,1,0:T(8,128)}), f32[8,2,32,16,128]{4,3,2,1,0:T(8,128)}, u32[]{:S(2)}, u32[]{:S(2)}) async-start(f32[8,2,32,16,128]{4,3,2,1,0:T(8,128)} %bins_prep.1), calls=%async_computation.1 | async-start | bytes 8388608 | tf_op jit(solution)/shard_map/all_to_all | solution.py:552
  19.1 21.4 %row_fft.1 = (f32[16,512,128]{2,1,0:T(8,128)}, f32[16,512,128]{2,1,0:T(8,128)}) custom-call(f32[1,512,4096]{2,1,0:T(8,128)} %map_ref.1, s32[512,4096]{1,0:T(8,128)} %mask_ref.1, f32[2,16,128]{2,1,0:T(8,128)} %constant.111.clone.turn_ref, bf16[2,256,256]{2,1,0:T(8,128)(2,1)} %constant.116.high_ref, bf16[2,256,256]{2,1,0:T(8,128)(2,1)} %constant.119.low_ref), custom_call_target="tpu_custom_call" | custom-call | tf_op jit(solution)/shard_map/row_fft/pallas_call | solution.py:561
  40.5 27.8 %all-to-all-done.1.bins0_ref.bins1_ref = f32[8,2,32,16,128]{4,3,2,1,0:T(8,128)} async-done(((f32[8,2,32,16,128]{4,3,2,1,0:T(8,128)}), f32[8,2,32,16,128]{4,3,2,1,0:T(8,128)}, u32[]{:S(2)}, u32[]{:S(2)}) %all-to-all-start.1) | async-done | bytes 4194336 | tf_op jit(solution)/shard_map/all_to_all | solution.py:552
  68.3 4.6 %all-to-all-start = ((f32[16,512,128]{2,1,0:T(8,128)}), f32[16,512,128]{2,1,0:T(8,128)}, u32[]{:S(2)}, u32[]{:S(2)}) async-start(f32[16,512,128]{2,1,0:T(8,128)} %get-tuple-element.10), calls=%async_computation | async-start | bytes 8388608 | tf_op jit(solution)/shard_map/all_to_all | solution.py:588
  73.1 52.1 %all-to-all-done = f32[16,512,128]{2,1,0:T(8,128)} async-done(((f32[16,512,128]{2,1,0:T(8,128)}), f32[16,512,128]{2,1,0:T(8,128)}, u32[]{:S(2)}, u32[]{:S(2)}) %all-to-all-start) | async-done | bytes 4194336 | tf_op jit(solution)/shard_map/all_to_all | solution.py:588
  125.2 6.9 %all-to-all-start.2 = ((f32[16,512,128]{2,1,0:T(8,128)}), f32[16,512,128]{2,1,0:T(8,128)}, u32[]{:S(2)}, u32[]{:S(2)}) async-start(f32[16,512,128]{2,1,0:T(8,128)} %get-tuple-element.12), calls=%async_computation.2 | async-start | bytes 8388608 | tf_op jit(solution)/shard_map/all_to_all | solution.py:588
  132.1 1.0 fusion.17
  134.3 0.7 pad_maximum_fusion.7
  135.7 72.1 %band_sums.2 = (f32[48,64]{1,0:T(8,128)S(1)}, f32[32,2,256]{2,1,0:T(2,128)S(1)}) custom-call(s32[3]{0:T(128)S(1)} %pad_add_fusion.info_ref, f32[8,2,512,128]{3,2,1,0:T(8,128)} %bitcast.2.x_ref, f32[8,2,32,16,128]{4,3,2,1,0:T(8,128)} %all-to-all-done.1.bins0_ref.bins1_ref, f32[8,2,32,16,128]{4,3,2,1,0:T(8,128)} %all-to-all-done.1.bins0_ref.bins1_ref, ...), custom_call_target="tpu_custom_call" | custom-call | tf_op jit(solution)/shard_map/band_sums/pallas_call | solution.py:601
  208.2 2.9 reverse.5
  212.1 0.6 broadcast_multiply_fusion
  213.2 72.7 %band_sums.3 = (f32[48,64]{1,0:T(8,128)S(1)}, f32[32,2,256]{2,1,0:T(2,128)}) custom-call(s32[3]{0:T(128)S(1)} %pad_add_fusion.2.info_ref, f32[8,2,512,128]{3,2,1,0:T(8,128)} %bitcast.7.x_ref, f32[8,2,32,16,128]{4,3,2,1,0:T(8,128)} %all-to-all-done.1.bins0_ref.bins1_ref, f32[8,2,32,16,128]{4,3,2,1,0:T(8,128)} %all-to-all-done.1.bins0_ref.bins1_ref, ...), custom_call_target="tpu_custom_call" | custom-call | tf_op jit(solution)/shard_map/band_sums/pallas_call | solution.py:601
  286.8 0.8 collective-permute-done
  287.7 1.9 collective-permute-start.1
  289.5 1.9 collective-permute-done.1
  291.4 1.9 collective-permute-start.2
  293.3 1.9 collective-permute-done.2
  295.2 1.9 collective-permute-start.3
  297.0 1.9 collective-permute-done.3
  299.0 3.4 %collective-permute-start.4 = (f32[3,1024]{1,0:T(4,128)S(1)}, f32[3,1024]{1,0:T(4,128)S(1)}, u32[]{:S(2)}, u32[]{:S(2)}) collective-permute-start(f32[3,1024]{1,0:T(4,128)S(1)} %add_multiply_fusion), channel_id=1, source_target_pairs={{0,2},{1,3},{2,0},{3,1},{4,6},{5,7},{6,4},{7,5},{8,10},{9,11},{10,... | collective-permute-start | bytes 36872 | tf_op jit(solution)/shard_map/ppermute | solution.py:19
  302.4 1.7 collective-permute-done.4
  304.1 0.6 copy.16
  (56 shorter events, 4.9 us)
Async XLA Ops:
  13.9 54.4 %all-to-all-start.1 = ((f32[8,2,32,16,128]{4,3,2,1,0:T(8,128)}), f32[8,2,32,16,128]{4,3,2,1,0:T(8,128)}, u32[]{:S(2)}, u32[]{:S(2)}) async-start(f32[8,2,32,16,128]{4,3,2,1,0:T(8,128)} %bins_prep.1), calls=%async_computation.1 | async-start | bytes 8388608 | tf_op jit(solution)/shard_map/all_to_all | solution.py:552
  68.3 56.8 %all-to-all-start = ((f32[16,512,128]{2,1,0:T(8,128)}), f32[16,512,128]{2,1,0:T(8,128)}, u32[]{:S(2)}, u32[]{:S(2)}) async-start(f32[16,512,128]{2,1,0:T(8,128)} %get-tuple-element.10), calls=%async_computation | async-start | bytes 8388608 | tf_op jit(solution)/shard_map/all_to_all | solution.py:588
  125.2 10.5 %copy-start = (f32[2,128,128]{2,1,0:T(8,128)S(1)}, f32[2,128,128]{2,1,0:T(8,128)}, u32[]{:S(2)}) copy-start(f32[2,128,128]{2,1,0:T(8,128)} %constant.112.clone.turn_ref) | copy-start | bytes 393220
  125.2 10.5 %copy-start.1 = (bf16[256,256]{1,0:T(8,128)(2,1)S(1)}, bf16[256,256]{1,0:T(8,128)(2,1)}, u32[]{:S(2)}) copy-start(bf16[256,256]{1,0:T(8,128)(2,1)} %constant.120.high_ref) | copy-start | bytes 393220
  125.2 10.5 %copy-start.2 = (bf16[256,256]{1,0:T(8,128)(2,1)S(1)}, bf16[256,256]{1,0:T(8,128)(2,1)}, u32[]{:S(2)}) copy-start(bf16[256,256]{1,0:T(8,128)(2,1)} %constant.123.low_ref) | copy-start | bytes 393220
  125.2 88.0 %all-to-all-start.2 = ((f32[16,512,128]{2,1,0:T(8,128)}), f32[16,512,128]{2,1,0:T(8,128)}, u32[]{:S(2)}, u32[]{:S(2)}) async-start(f32[16,512,128]{2,1,0:T(8,128)} %get-tuple-element.12), calls=%async_computation.2 | async-start | bytes 8388608 | tf_op jit(solution)/shard_map/all_to_all | solution.py:588
  135.6 75.9 %copy-start.3 = (f32[2]{0:T(128)S(1)}, f32[2]{0:T(128)}, u32[]{:S(2)}) copy-start(f32[2]{0:T(128)} %constant.124) | copy-start | bytes 28
  135.6 75.9 %copy-start.4 = (f32[2]{0:T(128)S(1)}, f32[2]{0:T(128)}, u32[]{:S(2)}) copy-start(f32[2]{0:T(128)} %constant.125) | copy-start | bytes 28
  213.2 85.7 %copy-start.5 = (f32[3]{0:T(128)S(1)}, f32[3]{0:T(128)}, u32[]{:S(2)}) copy-start(f32[3]{0:T(128)} %constant.114.clone) | copy-start | bytes 40
  286.5 1.2 collective-permute-start
  287.7 3.7 %collective-permute-start.1 = (f32[3,1024]{1,0:T(4,128)S(1)}, f32[3,1024]{1,0:T(4,128)S(1)}, u32[]{:S(2)}, u32[]{:S(2)}) collective-permute-start(f32[3,1024]{1,0:T(4,128)S(1)} %add.295), channel_id=1, source_target_pairs={{0,8},{4,12},{8,0},{12,4},{16,24},{20,28},{24,16},{28,20},{1,9},{5... | collective-permute-start | bytes 36872 | tf_op jit(solution)/shard_map/ppermute | solution.py:19
  291.4 3.7 %collective-permute-start.2 = (f32[3,1024]{1,0:T(4,128)S(1)}, f32[3,1024]{1,0:T(4,128)S(1)}, u32[]{:S(2)}, u32[]{:S(2)}) collective-permute-start(f32[3,1024]{1,0:T(4,128)S(1)} %add.296), channel_id=1, source_target_pairs={{0,16},{4,20},{8,24},{12,28},{16,0},{20,4},{24,8},{28,12},{1,17},{... | collective-permute-start | bytes 36872 | tf_op jit(solution)/shard_map/ppermute | solution.py:19
  295.2 3.7 %collective-permute-start.3 = (f32[3,1024]{1,0:T(4,128)S(1)}, f32[3,1024]{1,0:T(4,128)S(1)}, u32[]{:S(2)}, u32[]{:S(2)}) collective-permute-start(f32[3,1024]{1,0:T(4,128)S(1)} %add.297), channel_id=1, source_target_pairs={{0,1},{1,0},{2,3},{3,2},{4,5},{5,4},{6,7},{7,6},{8,9},{9,8},{10,11... | collective-permute-start | bytes 36872 | tf_op jit(solution)/shard_map/ppermute | solution.py:19
  299.0 5.1 %collective-permute-start.4 = (f32[3,1024]{1,0:T(4,128)S(1)}, f32[3,1024]{1,0:T(4,128)S(1)}, u32[]{:S(2)}, u32[]{:S(2)}) collective-permute-start(f32[3,1024]{1,0:T(4,128)S(1)} %add_multiply_fusion), channel_id=1, source_target_pairs={{0,2},{1,3},{2,0},{3,1},{4,6},{5,7},{6,4},{7,5},{8,10},{9,11},{10,... | collective-permute-start | bytes 36872 | tf_op jit(solution)/shard_map/ppermute | solution.py:19

commit v2 on v1

--- a/solution.py
+++ b/solution.py
@@ -196,6 +196,7 @@
 LANES = 128
 OUTER = 32
 HALF = LANES // 2
+SUB = LANES // 4
 GROUPS = 16
 LOWS = 64
 
@@ -261,24 +262,22 @@
     b = np.arange(LANES)[:, None]
     k = np.arange(LANES)[None, :]
     cosine, sine = wave_matrix(2 * np.pi * (b * k % LANES) / LANES)
-    top = np.concatenate([cosine, -sine], 1)
-    low = np.concatenate([sine, cosine], 1)
-    natural = np.concatenate([top, low], 0)
+    natural = np.concatenate(
+        [np.concatenate([cosine, -sine], 1), np.concatenate([sine, cosine], 1)], 0
+    )
+    first = np.zeros((2 * LANES, 2 * LANES))
+    first[:LANES, :HALF] = cosine[:, :HALF]
+    first[:LANES, LANES : LANES + HALF] = -sine[:, :HALF]
+    first[:LANES, LANES] = 1.0 - 2.0 * (np.arange(LANES) % 2)
+    freq = OUTER // 2 + OUTER * (HALF - 1 - np.arange(HALF)[None, :])
+    cosine, sine = wave_matrix(2 * np.pi * (b * freq % extent) / extent)
+    first[LANES:, HALF:LANES] = cosine
+    first[LANES:, LANES + HALF :] = -sine
     order = np.concatenate(
-        [np.arange(HALF), LANES + np.arange(HALF), HALF + np.arange(HALF), LANES + HALF + np.arange(HALF)]
-    )
-    family = natural[:, order]
-    first = np.zeros((2 * LANES, 2 * LANES))
-    i = np.arange(HALF)[None, :]
-    cosine, sine = wave_matrix(2 * np.pi * (b * i % LANES) / LANES)
-    first[:LANES, :HALF] = cosine
-    first[:LANES, HALF:LANES] = -sine
-    first[:LANES, HALF] = 1.0 - 2.0 * (np.arange(LANES) % 2)
-    freq = OUTER // 2 + OUTER * (HALF - 1 - i)
-    cosine, sine = wave_matrix(2 * np.pi * (b * freq % extent) / extent)
-    first[LANES:, LANES : LANES + HALF] = cosine
-    first[LANES:, LANES + HALF :] = -sine
-    return first, family, natural
+        [part + SUB * s + np.arange(SUB) for s in range(LANES // SUB) for part in (0, LANES)]
+    )
+    rows = np.concatenate([part + HALF * h + np.arange(HALF) for h in range(2) for part in (0, LANES)])
+    return first[:, order], natural[:, order], natural[rows]
 
 
 def split_table(table):
@@ -301,8 +300,11 @@
     return dot_f32(high, table_high) + (dot_f32(low, table_high) + dot_f32(high, table_low))
 
 
-def row_kernel(map_ref, mask_ref, turn_ref, high_ref, low_ref, out0_ref, out1_ref, mid_ref):
+def row_kernel(
+    map_ref, mask_ref, turn_ref, high_ref, low_ref, first_ref, second_ref, mid_ref
+):
     block = map_ref.shape[1]
+    left = lax.broadcasted_iota(jnp.int32, (block // 2, LANES), 1) < HALF
 
     def tile(step, carry):
         start = pl.multiple_of(step * 8, 8)
@@ -328,68 +330,85 @@
     def family(k, carry):
         which = jnp.minimum(k, 1)
         value = three_pass(mid_ref[k], high_ref[which], low_ref[which])
-        out0_ref[k] = value[:, :LANES]
-        out1_ref[k] = value[:, LANES:]
+        subs = []
+        for lanes in (slice(0, LANES), slice(LANES, 2 * LANES)):
+            top, low = value[: block // 2, lanes], value[block // 2 :, lanes]
+            subs.append(jnp.where(left, top, pltpu.roll(low, HALF, 1)))
+            subs.append(jnp.where(left, pltpu.roll(top, HALF, 1), low))
+        for index in range(2):
+            first_ref[k, index] = subs[index]
+            second_ref[k, index] = subs[2 + index]
         return carry
 
     lax.fori_loop(0, OUTER // 2, family, 0)
 
 
-def bins_kernel(info_ref, bins_ref, flip_ref, out_ref, both_ref):
+def bins_kernel(info_ref, bins_ref, flip_ref, out_ref, turn_ref):
     step = pl.program_id(0)
     sub = bins_ref.shape[1]
     parity = info_ref[0]
     upper = info_ref[1]
     dests = out_ref.shape[0]
     width = out_ref.shape[3]
+    zero = parity == 0
+    high_side = upper == 1
     for c in range(sub):
         kappa = step * sub + c
         mirrored = (OUTER - kappa) % OUTER
-        turned_bins = bins_ref[:, c, :].astype(jnp.float32).T
-        high = jnp.floor(turned_bins * 0.125)
-        low = turned_bins - high * 8.0
-        pair = jnp.concatenate([high.astype(jnp.bfloat16), low.astype(jnp.bfloat16)], 1)
-        both_ref[0] = turned_bins
-        both_ref[1] = dot_f32(pair, flip_ref[jnp.minimum(kappa, 1)])
-        for dest in range(dests):
-            fam = 2 * dest + parity
-            zero = fam == 0
-            col0 = jnp.where(zero & (upper == 1), OUTER // 2, fam)
-            rev0 = jnp.where(zero & (upper == 1), 1, 0)
-            col1 = jnp.where(zero, jnp.where(upper == 1, 0, OUTER // 2), OUTER - fam)
-            rev1 = jnp.where(zero & (upper == 0), 0, 1)
-            k0 = jnp.where(rev0 == 1, mirrored, kappa)
-            k1 = jnp.where(rev1 == 1, mirrored, kappa)
-            out_ref[dest, 0, k0] = both_ref[rev0, pl.ds(col0, width, stride=OUTER), :]
-            out_ref[dest, 1, k1] = both_ref[rev1, pl.ds(col1, width, stride=OUTER), :]
+        turn_ref[c % 2] = bins_ref[:, c, :].astype(jnp.float32).T
+
+        def column(at):
+            return turn_ref[c % 2, pl.ds(at, width, stride=OUTER), :]
+
+        ahead = [column(jnp.where(zero & high_side, OUTER // 2, parity))]
+        back = [column(jnp.where(zero, jnp.where(high_side, 0, OUTER // 2), OUTER - parity))]
+        for dest in range(1, dests):
+            ahead.append(column(2 * dest + parity))
+            back.append(column(OUTER - 2 * dest - parity))
+        mixed = jnp.concatenate([ahead[0]] + back, 0)
+        high = jnp.floor(mixed * 0.125)
+        pair = jnp.concatenate([high.astype(jnp.bfloat16), (mixed - high * 8.0).astype(jnp.bfloat16)], 1)
+        flipped = dot_f32(pair, flip_ref[jnp.minimum(kappa, 1)])
+        turn0 = zero & high_side
+        turn1 = jnp.logical_not(zero & jnp.logical_not(high_side))
+        out_ref[0, 0, jnp.where(turn0, mirrored, kappa)] = jnp.where(turn0, flipped[:width], ahead[0])
+        out_ref[0, 1, jnp.where(turn1, mirrored, kappa)] = jnp.where(
+            turn1, flipped[width : 2 * width], back[0]
+        )
+        for dest in range(1, dests):
+            out_ref[dest, 0, kappa] = ahead[dest]
+            out_ref[dest, 1, mirrored] = flipped[(dest + 1) * width : (dest + 2) * width]
 
 
 def band_kernel(
-    extent, nbins, chunk, info_ref, x_ref, bins0_ref, bins1_ref, turn_ref, high_ref, low_ref, fx_ref,
-    sums_ref, edge_ref, mid_ref, power_ref, part_ref,
+    extent, with_edge, info_ref, x_ref, bins0_ref, bins1_ref, turn_ref, high_ref, low_ref,
+    fx_ref, *refs,
 ):
+    if with_edge:
+        sums_ref, edge_ref, mid_ref, power_ref, part_ref = refs
+    else:
+        sums_ref, mid_ref, power_ref, part_ref = refs
+    sub = pl.program_id(0)
     offset = info_ref[0]
     flipped = info_ref[1]
-    hollow = info_ref[2]
-    local = x_ref.shape[2]
-    per_slab = local // LANES
-    lane8 = lax.broadcasted_iota(jnp.int32, (8, LANES), 1)
-    left8 = lane8 < HALF
+    hollow = (info_ref[2] == 1) & (sub == 0)
+    per_slab = x_ref.shape[3] // HALF
+    even8 = lax.broadcasted_iota(jnp.int32, (8, LANES), 1) % HALF < SUB
 
     def tile(step, carry):
         start = pl.multiple_of(step * 8, 8)
         cells = []
         for a in range(OUTER):
-            rows = pl.ds((a % per_slab) * LANES + start, 8)
-            q = x_ref[a // per_slab, 0, rows, :]
-            u = x_ref[a // per_slab, 1, rows, :]
-            real = jnp.where(left8, q, pltpu.roll(u, HALF, 1))
-            imag = jnp.where(left8, pltpu.roll(q, HALF, 1), u)
+            rows = pl.ds((a % per_slab) * HALF + start, 8)
+            q = x_ref[a // per_slab, 0, 0, rows, :]
+            u = x_ref[a // per_slab, 1, 0, rows, :]
+            real = jnp.where(even8, q, pltpu.roll(u, SUB, 1))
+            imag = jnp.where(even8, pltpu.roll(q, LANES - SUB, 1), u)
             cells.append((real, imag))
         waves = complex_fft(cells)
         turns = {1: (turn_ref[0, pl.ds(start, 8), :], turn_ref[1, pl.ds(start, 8), :])}
         mid_ref[0, pl.ds(start, 8), :] = waves[0][0]
-        mid_ref[0, pl.ds(LANES + start, 8), :] = waves[0][1]
+        mid_ref[0, pl.ds(HALF + start, 8), :] = waves[0][1]
         for k in range(1, OUTER):
             if k not in turns:
                 (ar, ai), (br, bi) = turns[k // 2], turns[k - k // 2]
@@ -397,93 +416,99 @@
             cosine, sine = turns[k]
             real, imag = waves[k]
             mid_ref[k, pl.ds(start, 8), :] = real * cosine - imag * sine
-            mid_ref[k, pl.ds(LANES + start, 8), :] = real * sine + imag * cosine
+            mid_ref[k, pl.ds(HALF + start, 8), :] = real * sine + imag * cosine
         return carry
 
-    lax.fori_loop(0, LANES // 8, tile, 0)
-
-    fx = fx_ref[...]
-    lane = lax.broadcasted_iota(jnp.int32, (HALF, LANES), 1)
-    slot = lax.broadcasted_iota(jnp.int32, (HALF, LANES), 0)
-    keep = jnp.where((slot == 0) & (hollow == 1), 0.0, 1.0)
+    lax.fori_loop(0, HALF // 8, tile, 0)
+
+    fx = fx_ref[0]
+    lane = lax.broadcasted_iota(jnp.int32, (SUB, LANES), 1)
+    slot = lax.broadcasted_iota(jnp.int32, (SUB, LANES), 0)
+    keep = jnp.where((slot == 0) & hollow, 0.0, 1.0)
     inv_area = 1.0 / (extent * extent)
     group_iota = lax.broadcasted_iota(jnp.int32, (GROUPS, LANES), 0).astype(jnp.float32).astype(jnp.bfloat16)
     low_iota = lax.broadcasted_iota(jnp.int32, (LOWS, LANES), 0).astype(jnp.float32).astype(jnp.bfloat16)
     width = bins0_ref.shape[3]
+    near = SUB // width
     one = jnp.ones((LOWS, LANES), jnp.bfloat16)
     none = jnp.zeros((LOWS, LANES), jnp.bfloat16)
     empty = jnp.zeros((GROUPS, LANES), jnp.bfloat16)
-    unroll = 8
-
-    def family(k, acc):
-        spectrum = three_pass(mid_ref[k].T, high_ref[...], low_ref[...])
-        if chunk == 0:
-            edge_ref[k, 0:1, :] = spectrum[0:1, :]
-            edge_ref[k, 1:2, :] = spectrum[HALF : HALF + 1, :]
-        q_real, q_imag = spectrum[:HALF, :LANES], spectrum[:HALF, LANES:]
-        u_real, u_imag = spectrum[HALF:, :LANES], spectrum[HALF:, LANES:]
-        row = lane * OUTER + k
-        fy = jnp.where(row >= extent // 2, row - extent, row).astype(jnp.float32)
-        radius = jnp.maximum(fx * fx + fy * fy, 1.0)
-        cos_twice = (fx * fx - fy * fy) / radius
-        sin_twice = 2.0 * fx * fy / radius
-
-        def powers(sine, which):
-            e_real = cos_twice * q_real + sine * u_real
-            e_imag = cos_twice * q_imag + sine * u_imag
-            b_real = cos_twice * u_real - sine * q_real
-            b_imag = cos_twice * u_imag - sine * q_imag
-            power_ref[which, 0] = (e_real * e_real + e_imag * e_imag) * inv_area * keep
-            power_ref[which, 1] = (b_real * b_real + b_imag * b_imag) * inv_area * keep
-            power_ref[which, 2] = (e_real * b_real + e_imag * b_imag) * inv_area * keep
-
-        other = jnp.where(k == 0, 1, 0)
-        powers(sin_twice, jnp.where(k == 0, 1 - flipped, 0))
-
-        @pl.when(k == 0)
-        def _():
-            powers(jnp.where(row == extent // 2, -sin_twice, sin_twice), flipped)
-
-        for index, bins_ref in enumerate((bins0_ref, bins1_ref)):
-            for source in range(bins_ref.shape[0]):
-                value = bins_ref[source, 0, k]
-                high = jnp.floor(value * (1.0 / LOWS))
-                part_ref[index, 0, source * width : (source + 1) * width] = high
-                part_ref[index, 1, source * width : (source + 1) * width] = value - high * LOWS
-
-        def slots(step, acc):
-            weighted, lows = [], []
-            for inner in range(unroll):
-                i = step * unroll + inner
-                mirror = (offset - i) & (HALF - 1)
+    begin0 = sub * near
+    begin1 = (1 - sub) * near
+
+    def pair(step, acc):
+        turned_rows = []
+        for member in range(2):
+            flat = mid_ref[2 * step + member].T
+            turned_rows.append(jnp.concatenate([flat[:HALF], flat[HALF:]], 1))
+        spectra = three_pass(jnp.concatenate(turned_rows, 0), high_ref[...], low_ref[...])
+        weighted, lows = [], []
+        for member in range(2):
+            k = 2 * step + member
+            spectrum = spectra[member * HALF : (member + 1) * HALF]
+            if with_edge:
+                edge_ref[sub, k, 0:1, :] = spectrum[0:1, :]
+                edge_ref[sub, k, 1:2, :] = spectrum[SUB : SUB + 1, :]
+            q_real, q_imag = spectrum[:SUB, :LANES], spectrum[:SUB, LANES:]
+            u_real, u_imag = spectrum[SUB:, :LANES], spectrum[SUB:, LANES:]
+            row = lane * OUTER + k
+            fy = jnp.where(row >= extent // 2, row - extent, row).astype(jnp.float32)
+            radius = jnp.maximum(fx * fx + fy * fy, 1.0)
+            cos_twice = (fx * fx - fy * fy) / radius
+            sin_twice = 2.0 * fx * fy / radius
+
+            def powers(sine, which):
+                e_real = cos_twice * q_real + sine * u_real
+                e_imag = cos_twice * q_imag + sine * u_imag
+                b_real = cos_twice * u_real - sine * q_real
+                b_imag = cos_twice * u_imag - sine * q_imag
+                power_ref[member, which, 0] = (e_real * e_real + e_imag * e_imag) * inv_area * keep
+                power_ref[member, which, 1] = (b_real * b_real + b_imag * b_imag) * inv_area * keep
+                power_ref[member, which, 2] = (e_real * b_real + e_imag * b_imag) * inv_area * keep
+
+            other = 0
+            if member == 0:
+                other = jnp.where(k == 0, 1, 0)
+                powers(sin_twice, jnp.where(k == 0, 1 - flipped, 0))
+
+                @pl.when(k == 0)
+                def _():
+                    powers(jnp.where(row == extent // 2, -sin_twice, sin_twice), flipped)
+
+            else:
+                powers(sin_twice, 0)
+
+            for index, (bins_ref, begin, count) in enumerate(
+                ((bins0_ref, begin0, near), (bins1_ref, begin1, near + 1))
+            ):
+                for source in range(count):
+                    at = jnp.minimum(begin + source, bins_ref.shape[0] - 1)
+                    value = bins_ref[at, 0, k]
+                    high = jnp.floor(value * (1.0 / LOWS))
+                    rows = slice(source * width, (source + 1) * width)
+                    part_ref[member, index, 0, rows] = high
+                    part_ref[member, index, 1, rows] = value - high * LOWS
+
+            for i in range(SUB):
+                mirror = offset - HALF + SUB - i
                 for index, at, source in ((0, i, 0), (1, mirror, other)):
-                    def line(ref, *where_):
-                        return ref[where_ + (pl.ds(at, 1), slice(None))]
-                    high = part_ref[index, 0, pl.ds(at, 1), :]
-                    low = part_ref[index, 1, pl.ds(at, 1), :]
+                    high = part_ref[member, index, 0, pl.ds(at, 1), :]
+                    low = part_ref[member, index, 1, pl.ds(at, 1), :]
                     high = jnp.broadcast_to(high, (GROUPS, LANES)).astype(jnp.bfloat16)
                     low = jnp.broadcast_to(low, (LOWS, LANES)).astype(jnp.bfloat16)
                     hot = high == group_iota
                     column = []
                     for kind in range(3):
-                        power = power_ref[source, kind, pl.ds(i, 1), :]
+                        power = power_ref[member, source, kind, pl.ds(i, 1), :]
                         power = jnp.broadcast_to(power, (GROUPS, LANES)).astype(jnp.bfloat16)
                         column.append(jnp.where(hot, power, empty))
                     weighted.append(jnp.concatenate(column, 0))
                     lows.append(jnp.where(low == low_iota, one, none))
-            return acc + dot_f32(
-                jnp.concatenate(weighted, 1), jnp.concatenate(lows, 1), (((1,), (1,)), ((), ()))
-            )
-
-        return lax.fori_loop(0, HALF // unroll, slots, acc)
-
-    sums_ref[...] = lax.fori_loop(0, OUTER, family, jnp.zeros((3 * GROUPS, LOWS), jnp.float32))
-
-
-def vmem_spec(*block):
-    if block:
-        return pl.BlockSpec(*block)
-    return pl.BlockSpec(memory_space=pltpu.VMEM)
+        return acc + dot_f32(
+            jnp.concatenate(weighted, 1), jnp.concatenate(lows, 1), (((1,), (1,)), ((), ()))
+        )
+
+    sums_ref[0] = lax.fori_loop(0, OUTER // 2, pair, jnp.zeros((3 * GROUPS, LOWS), jnp.float32))
 
 
 def summed(array, axis):
@@ -556,8 +581,8 @@
     angles = 2 * np.pi * (k1 * np.arange(LANES)[None, :] % extent) / extent
     turns = jnp.asarray(np.stack([np.cos(angles), -np.sin(angles)]), jnp.float32)
     table_spec = pl.BlockSpec((2, 2 * LANES, 2 * LANES), lambda i: (0, 0, 0))
-    piece = jax.ShapeDtypeStruct((2 * slabs, count, LANES), jnp.float32)
-    piece_spec = pl.BlockSpec((2 * slabs, block, LANES), lambda i: (0, i, 0))
+    piece = jax.ShapeDtypeStruct((2 * slabs, 2, count // 2, LANES), jnp.float32)
+    piece_spec = pl.BlockSpec((2 * slabs, 2, block // 2, LANES), lambda i: (0, 0, i, 0))
     pieces = pl.pallas_call(
         row_kernel,
         grid=(count // block,),
@@ -579,57 +604,60 @@
         for sky in range(reps // 2)
     ]
     fam = 2 * slab_index + pair_bit
-    angles = 2 * np.pi * np.arange(LANES) / extent
-    spin = np.stack([np.cos(angles), -np.sin(angles)])[:, :, None]
-    spin = jnp.asarray(np.broadcast_to(spin, (2, LANES, LANES)), jnp.float32)
+    angles = np.arange(HALF)[:, None] + HALF * (np.arange(LANES)[None, :] >= HALF)
+    angles = 2 * np.pi * angles / extent
+    spin = jnp.asarray(np.stack([np.cos(angles), -np.sin(angles)]), jnp.float32)
     slots = lax.iota(jnp.int32, HALF)
+    zero = (fam == 0).astype(jnp.int32)
     total = None
-    for chunk in range(2):
+    for chunk, piece in enumerate(pieces):
         got = lax.all_to_all(
-            pieces[chunk], ("rows", "rep"), split_axis=0, concat_axis=0, tiled=True,
+            piece, ("rows", "rep"), split_axis=0, concat_axis=0, tiled=True,
             axis_index_groups=groups,
-        ).reshape(slabs, 2, count, LANES)
+        ).reshape(slabs, 2, -1, count // 2, LANES)
+        subs = got.shape[2]
         first_col = OUTER * slots if chunk == 0 else OUTER // 2 + OUTER * (HALF - 1 - slots)
         col = jnp.where(fam == 0, first_col, fam + OUTER * (slots + HALF * chunk))
-        fx = jnp.broadcast_to(signed_float(col, extent)[:, None], (HALF, LANES))
-        zero = (fam == 0).astype(jnp.int32)
-        if chunk == 0:
+        fx = jnp.broadcast_to(signed_float(col, extent).reshape(subs, SUB, 1), (subs, SUB, LANES))
+        with_edge = chunk == 0
+        if with_edge:
             info = jnp.stack([HALF - 1 + zero, jnp.int32(1), zero])
         else:
             info = jnp.stack([jnp.int32(HALF - 1), 1 - zero, jnp.int32(0)])
         bin_block = (half_slabs, 1, OUTER, width, LANES)
-        sums, edge = pl.pallas_call(
-            functools.partial(band_kernel, extent, NBINS, chunk),
-            grid=(1,),
+        edge_shape = (subs, OUTER, 2, 2 * LANES)
+        sums_shape = (subs, 3 * GROUPS, LOWS)
+        out = pl.pallas_call(
+            functools.partial(band_kernel, extent, with_edge),
+            grid=(subs,),
             in_specs=[
                 pl.BlockSpec(memory_space=pltpu.SMEM),
-                pl.BlockSpec(got.shape, lambda i: (0, 0, 0, 0)),
+                pl.BlockSpec((slabs, 2, 1, count // 2, LANES), lambda i: (0, 0, i, 0, 0)),
                 pl.BlockSpec(bin_block, lambda i, at=chunk: (at, 0, 0, 0, 0)),
                 pl.BlockSpec(bin_block, lambda i, at=1 - chunk: (at, 1, 0, 0, 0)),
                 pl.BlockSpec(spin.shape, lambda i: (0, 0, 0)),
                 pl.BlockSpec(col_high.shape, lambda i: (0, 0)),
                 pl.BlockSpec(col_low.shape, lambda i: (0, 0)),
-                pl.BlockSpec(fx.shape, lambda i: (0, 0)),
+                pl.BlockSpec((1, SUB, LANES), lambda i: (i, 0, 0)),
             ],
-            out_specs=[
-                pl.BlockSpec((3 * GROUPS, LOWS), lambda i: (0, 0)),
-                pl.BlockSpec((OUTER, 2, 2 * LANES), lambda i: (0, 0, 0)),
-            ],
-            out_shape=[
-                jax.ShapeDtypeStruct((3 * GROUPS, LOWS), jnp.float32),
-                jax.ShapeDtypeStruct((OUTER, 2, 2 * LANES), jnp.float32),
-            ],
+            out_specs=[pl.BlockSpec((1, 3 * GROUPS, LOWS), lambda i: (i, 0, 0))]
+            + [pl.BlockSpec(edge_shape, lambda i: (0, 0, 0, 0))] * with_edge,
+            out_shape=[jax.ShapeDtypeStruct(sums_shape, jnp.float32)]
+            + [jax.ShapeDtypeStruct(edge_shape, jnp.float32)] * with_edge,
             scratch_shapes=[
-                pltpu.VMEM((OUTER, 2 * LANES, LANES), jnp.float32),
-                pltpu.VMEM((2, 3, HALF, LANES), jnp.float32),
-                pltpu.VMEM((2, 2, HALF, LANES), jnp.float32),
+                pltpu.VMEM((OUTER, LANES, LANES), jnp.float32),
+                pltpu.VMEM((2, 2, 3, SUB, LANES), jnp.float32),
+                pltpu.VMEM((2, 2, 2, SUB + width, LANES), jnp.float32),
             ],
             compiler_params=pltpu.CompilerParams(vmem_limit_bytes=48 * 2**20),
             name="band_sums",
         )(info, got, got_bins, got_bins, spin, col_high, col_low, fx)
+        sums = out[0].sum(0)
         total = sums if total is None else total + sums
-        if chunk == 0:
-            special = edge_sums(edge, got_bins[0, 0, :, 0], got_bins[half_slabs, 1, :, 0], extent)
+        if with_edge:
+            special = edge_sums(
+                out[1][0], got_bins[0, 0, :, 0], got_bins[half_slabs, 1, :, 0], extent
+            )
             special = jnp.where(fam == 0, special, 0.0)
     partial_sums = total.reshape(3, NBINS) + special
     auto = NBINS / (extent * extent)

time: 305 us -> 244 us (0.80)
  Pallas kernels: 179 us -> 119 us
    pallas_call x2, Pallas kernels: 145 us -> 81.1 us  [on_device_fast(): pl.pallas_call(functools.partial(band_kernel, extent, with_edge), grid=(s...]
    pallas_call x1, Pallas kernels: 21.4 us -> 27 us  [on_device_fast(): pl.pallas_call(row_kernel, grid=(count // block,), in_specs=[pl.BlockSpec...]
    all_to_all x1, waiting for transfers between devices: 27.8 us -> 22.2 us  [on_device_fast(): lax.all_to_all(sent_bins, 'rows', split_axis=0, concat_axis=0, tiled=True)]
    all_to_all x2, waiting for transfers between devices: 52.1 us -> 55.5 us  [on_device_fast(): lax.all_to_all(piece, ('rows', 'rep'), split_axis=0, concat_axis=0, tiled...]
  transfers between devices with their start and end apart: 8 -> 8, of which waited for: 7 -> 8; matrix products, arithmetic and copies ran while one was open for 3% -> 4% of each run, Pallas kernels for 31% -> 28%
where the time goes in v2:
time: 244 us
  Pallas kernels  119 us (49%)
  waiting for transfers between devices  87.3 us (36%)
  starting transfers between devices  25.7 us (11%)
  local copies, waits for them, and re-layouts  6.96 us (3%)
  other arithmetic  3.59 us (1%)
    pallas_call x2, Pallas kernels, on_device_fast(): pl.pallas_call(functools.partial(band_kernel, extent, with_edge), grid=(s...  81.1 us
    all_to_all x2, waiting for transfers between devices, on_device_fast(): lax.all_to_all(piece, ('rows', 'rep'), split_axis=0, concat_axis=0, tiled...  55.5 us
    pallas_call x1, Pallas kernels, on_device_fast(): pl.pallas_call(row_kernel, grid=(count // block,), in_specs=[pl.BlockSpec...  27 us
    all_to_all x1, waiting for transfers between devices, on_device_fast(): lax.all_to_all(sent_bins, 'rows', split_axis=0, concat_axis=0, tiled=True)  22.2 us
    all_to_all x2, starting transfers between devices, on_device_fast(): lax.all_to_all(piece, ('rows', 'rep'), split_axis=0, concat_axis=0, tiled...  11.5 us
    pallas_call x1, Pallas kernels, on_device_fast(): pl.pallas_call(bins_kernel, grid=(OUTER // sub,), in_specs=[pl.BlockSpec(...  11 us
    ppermute x5, waiting for transfers between devices, partner(): lax.ppermute(array, axis, [(i, i ^ 1 << distance) for i in range(lax.axis...  9.64 us
    ppermute x5, starting transfers between devices, partner(): lax.ppermute(array, axis, [(i, i ^ 1 << distance) for i in range(lax.axis...  9.05 us
  transfers between devices with their start and end apart: 8, of which 8 were waited for; matrix products, arithmetic and copies ran while one was open for 4% of the time, Pallas kernels for 28%

profile of v2, /device:TPU:0, one launch (start us, length us, event | category | flops | bytes accessed | tf_op | source)
XLA Modules:
  0.0 243.5 jit_solution(11339279784855741410)
XLA Ops:
  0.0 0.7 pad_add_fusion.1.info_ref
  0.7 11.0 %bins_prep.1 = f32[8,2,32,16,128]{4,3,2,1,0:T(8,128)} custom-call(s32[2]{0:T(128)} %pad_add_fusion.1.info_ref, s32[128,32,512]{2,1,0:T(8,128)} %bitcast.31, bf16[2,256,128]{2,1,0:T(8,128)(2,1)} %constant.113.clone.flip_ref), custom_call_target="tpu_custom_call" | custom-call | tf_op jit(solution)/shard_map/bins_prep/pallas_call | solution.py:564
  11.7 5.2 %all-to-all-start.1 = ((f32[8,2,32,16,128]{4,3,2,1,0:T(8,128)}), f32[8,2,32,16,128]{4,3,2,1,0:T(8,128)}, u32[]{:S(2)}, u32[]{:S(2)}) async-start(f32[8,2,32,16,128]{4,3,2,1,0:T(8,128)} %bins_prep.1), calls=%async_computation.1 | async-start | bytes 8388608 | tf_op jit(solution)/shard_map/all_to_all | solution.py:577
  16.9 27.0 %row_fft.1 = (f32[16,2,256,128]{3,2,1,0:T(8,128)}, f32[16,2,256,128]{3,2,1,0:T(8,128)}) custom-call(f32[1,512,4096]{2,1,0:T(8,128)} %map_ref.1, s32[512,4096]{1,0:T(8,128)} %mask_ref.1, f32[2,16,128]{2,1,0:T(8,128)} %constant.114.clone.turn_ref, bf16[2,256,256]{2,1,0:T(8,128)(2,1)} %constant.119.high_ref, bf16[2,256,256]{2,1,0:T(8,128)(2,1)} %constant.122.low_ref), custom_call_target="tpu_custom_call" | custom-call | tf_op jit(solution)/shard_map/row_fft/pallas_call | solution.py:586
  43.9 22.2 %all-to-all-done.1.bins0_ref.bins1_ref = f32[8,2,32,16,128]{4,3,2,1,0:T(8,128)} async-done(((f32[8,2,32,16,128]{4,3,2,1,0:T(8,128)}), f32[8,2,32,16,128]{4,3,2,1,0:T(8,128)}, u32[]{:S(2)}, u32[]{:S(2)}) %all-to-all-start.1) | async-done | bytes 4194336 | tf_op jit(solution)/shard_map/all_to_all | solution.py:577
  66.1 4.6 %all-to-all-start = ((f32[16,2,256,128]{3,2,1,0:T(8,128)}), f32[16,2,256,128]{3,2,1,0:T(8,128)}, u32[]{:S(2)}, u32[]{:S(2)}) async-start(f32[16,2,256,128]{3,2,1,0:T(8,128)} %get-tuple-element.9), calls=%async_computation | async-start | bytes 8388608 | tf_op jit(solution)/shard_map/all_to_all | solution.py:614
  70.8 1.0 fusion.17
  73.1 49.8 %all-to-all-done = f32[16,2,256,128]{3,2,1,0:T(8,128)} async-done(((f32[16,2,256,128]{3,2,1,0:T(8,128)}), f32[16,2,256,128]{3,2,1,0:T(8,128)}, u32[]{:S(2)}, u32[]{:S(2)}) %all-to-all-start) | async-done | bytes 4194336 | tf_op jit(solution)/shard_map/all_to_all | solution.py:614
  122.9 6.9 %all-to-all-start.2 = ((f32[16,2,256,128]{3,2,1,0:T(8,128)}), f32[16,2,256,128]{3,2,1,0:T(8,128)}, u32[]{:S(2)}, u32[]{:S(2)}) async-start(f32[16,2,256,128]{3,2,1,0:T(8,128)} %get-tuple-element.11), calls=%async_computation.2 | async-start | bytes 8388608 | tf_op jit(solution)/shard_map/all_to_all | solution.py:614
  129.8 0.7 pad_maximum_fusion.7
  131.2 40.6 %band_sums.2 = (f32[2,48,64]{2,1,0:T(8,128)S(1)}, f32[2,32,2,256]{3,2,1,0:T(2,128)S(1)}) custom-call(s32[3]{0:T(128)S(1)} %pad_add_fusion.info_ref, f32[8,2,2,256,128]{4,3,2,1,0:T(8,128)} %bitcast.2.x_ref, f32[8,2,32,16,128]{4,3,2,1,0:T(8,128)} %all-to-all-done.1.bins0_ref.bins1_ref, f32[8,2,32,16,128]{4,3,2,1,0:T(8,128)} %all-to-all-done.1.bins0_ref.bins1_ref, ...), custom_call_target="tpu_custom_call" | custom-call | tf_op jit(solution)/shard_map/band_sums/pallas_call | solution.py:630
  172.3 2.9 %reverse.5 = f32[2,2,4096]{2,1,0:T(2,128)S(1)} reverse(f32[2,2,4096]{2,1,0:T(2,128)S(1)} %bitcast.34), dimensions={2} | reverse | bytes 131072
  177.3 5.6 %all-to-all-done.2 = f32[16,2,256,128]{3,2,1,0:T(8,128)} async-done(((f32[16,2,256,128]{3,2,1,0:T(8,128)}), f32[16,2,256,128]{3,2,1,0:T(8,128)}, u32[]{:S(2)}, u32[]{:S(2)}) %all-to-all-start.2) | async-done | bytes 4194336 | tf_op jit(solution)/shard_map/all_to_all | solution.py:614
  183.0 40.5 %band_sums.3 = f32[2,48,64]{2,1,0:T(8,128)S(1)} custom-call(s32[3]{0:T(128)S(1)} %pad_add_fusion.2.info_ref, f32[8,2,2,256,128]{4,3,2,1,0:T(8,128)} %bitcast.7.x_ref, f32[8,2,32,16,128]{4,3,2,1,0:T(8,128)} %all-to-all-done.1.bins0_ref.bins1_ref, f32[8,2,32,16,128]{4,3,2,1,0:T(8,128)} %all-to-all-done.1.bins0_ref.bins1_ref, f32[2,64,128]{2,1,0:T(8,128)S(1)} %copy-done.2, ...), custom_call_target="tpu_custom_call" | custom-call | tf_op jit(solution)/shard_map/band_sums/pallas_call | solution.py:630
  224.1 1.2 collective-permute-done
  225.3 1.4 collective-permute-start.1
  226.7 2.3 collective-permute-done.1
  229.0 1.0 collective-permute-start.2
  230.0 2.7 %collective-permute-done.2 = f32[3,1024]{1,0:T(4,128)S(1)} collective-permute-done((f32[3,1024]{1,0:T(4,128)S(1)}, f32[3,1024]{1,0:T(4,128)S(1)}, u32[]{:S(2)}, u32[]{:S(2)}) %collective-permute-start.2) | collective-permute-done | bytes 12320 | tf_op jit(solution)/shard_map/ppermute | solution.py:19
  232.8 3.2 %collective-permute-start.3 = (f32[3,1024]{1,0:T(4,128)S(1)}, f32[3,1024]{1,0:T(4,128)S(1)}, u32[]{:S(2)}, u32[]{:S(2)}) collective-permute-start(f32[3,1024]{1,0:T(4,128)S(1)} %add.307), channel_id=1, source_target_pairs={{0,1},{1,0},{2,3},{3,2},{4,5},{5,4},{6,7},{7,6},{8,9},{9,8},{10,11... | collective-permute-start | bytes 36872 | tf_op jit(solution)/shard_map/ppermute | solution.py:19
  236.0 1.7 collective-permute-done.3
  237.8 3.4 %collective-permute-start.4 = (f32[3,1024]{1,0:T(4,128)S(1)}, f32[3,1024]{1,0:T(4,128)S(1)}, u32[]{:S(2)}, u32[]{:S(2)}) collective-permute-start(f32[3,1024]{1,0:T(4,128)S(1)} %add_multiply_fusion), channel_id=1, source_target_pairs={{0,2},{1,3},{2,0},{3,1},{4,6},{5,7},{6,4},{7,5},{8,10},{9,11},{10,... | collective-permute-start | bytes 36872 | tf_op jit(solution)/shard_map/ppermute | solution.py:19
  241.1 1.7 collective-permute-done.4
  242.9 0.6 copy.16
  (59 shorter events, 5.2 us)
Async XLA Ops:
  11.7 54.4 %all-to-all-start.1 = ((f32[8,2,32,16,128]{4,3,2,1,0:T(8,128)}), f32[8,2,32,16,128]{4,3,2,1,0:T(8,128)}, u32[]{:S(2)}, u32[]{:S(2)}) async-start(f32[8,2,32,16,128]{4,3,2,1,0:T(8,128)} %bins_prep.1), calls=%async_computation.1 | async-start | bytes 8388608 | tf_op jit(solution)/shard_map/all_to_all | solution.py:577
  66.1 56.8 %all-to-all-start = ((f32[16,2,256,128]{3,2,1,0:T(8,128)}), f32[16,2,256,128]{3,2,1,0:T(8,128)}, u32[]{:S(2)}, u32[]{:S(2)}) async-start(f32[16,2,256,128]{3,2,1,0:T(8,128)} %get-tuple-element.9), calls=%async_computation | async-start | bytes 8388608 | tf_op jit(solution)/shard_map/all_to_all | solution.py:614
  122.9 8.2 %copy-start = (bf16[256,256]{1,0:T(8,128)(2,1)S(1)}, bf16[256,256]{1,0:T(8,128)(2,1)}, u32[]{:S(2)}) copy-start(bf16[256,256]{1,0:T(8,128)(2,1)} %constant.123.high_ref) | copy-start | bytes 393220
  122.9 8.2 %copy-start.1 = (bf16[256,256]{1,0:T(8,128)(2,1)S(1)}, bf16[256,256]{1,0:T(8,128)(2,1)}, u32[]{:S(2)}) copy-start(bf16[256,256]{1,0:T(8,128)(2,1)} %constant.126.low_ref) | copy-start | bytes 393220
  122.9 8.2 %copy-start.2 = (f32[2,64,128]{2,1,0:T(8,128)S(1)}, f32[2,64,128]{2,1,0:T(8,128)}, u32[]{:S(2)}) copy-start(f32[2,64,128]{2,1,0:T(8,128)} %constant.115.clone.turn_ref) | copy-start | bytes 196612
  122.9 60.0 %all-to-all-start.2 = ((f32[16,2,256,128]{3,2,1,0:T(8,128)}), f32[16,2,256,128]{3,2,1,0:T(8,128)}, u32[]{:S(2)}, u32[]{:S(2)}) async-start(f32[16,2,256,128]{3,2,1,0:T(8,128)} %get-tuple-element.11), calls=%async_computation.2 | async-start | bytes 8388608 | tf_op jit(solution)/shard_map/all_to_all | solution.py:614
  131.2 44.5 %copy-start.3 = (f32[2]{0:T(128)S(1)}, f32[2]{0:T(128)}, u32[]{:S(2)}) copy-start(f32[2]{0:T(128)} %constant.127) | copy-start | bytes 28
  131.2 44.5 %copy-start.4 = (f32[2]{0:T(128)S(1)}, f32[2]{0:T(128)}, u32[]{:S(2)}) copy-start(f32[2]{0:T(128)} %constant.128) | copy-start | bytes 28
  183.0 54.7 %copy-start.5 = (f32[3]{0:T(128)S(1)}, f32[3]{0:T(128)}, u32[]{:S(2)}) copy-start(f32[3]{0:T(128)} %constant.117.clone) | copy-start | bytes 40
  224.1 1.2 collective-permute-start
  225.3 3.7 %collective-permute-start.1 = (f32[3,1024]{1,0:T(4,128)S(1)}, f32[3,1024]{1,0:T(4,128)S(1)}, u32[]{:S(2)}, u32[]{:S(2)}) collective-permute-start(f32[3,1024]{1,0:T(4,128)S(1)} %add.305), channel_id=1, source_target_pairs={{0,8},{4,12},{8,0},{12,4},{16,24},{20,28},{24,16},{28,20},{1,9},{5... | collective-permute-start | bytes 36872 | tf_op jit(solution)/shard_map/ppermute | solution.py:19
  229.0 3.7 %collective-permute-start.2 = (f32[3,1024]{1,0:T(4,128)S(1)}, f32[3,1024]{1,0:T(4,128)S(1)}, u32[]{:S(2)}, u32[]{:S(2)}) collective-permute-start(f32[3,1024]{1,0:T(4,128)S(1)} %add.306), channel_id=1, source_target_pairs={{0,16},{4,20},{8,24},{12,28},{16,0},{20,4},{24,8},{28,12},{1,17},{... | collective-permute-start | bytes 36872 | tf_op jit(solution)/shard_map/ppermute | solution.py:19
  232.8 4.9 %collective-permute-start.3 = (f32[3,1024]{1,0:T(4,128)S(1)}, f32[3,1024]{1,0:T(4,128)S(1)}, u32[]{:S(2)}, u32[]{:S(2)}) collective-permute-start(f32[3,1024]{1,0:T(4,128)S(1)} %add.307), channel_id=1, source_target_pairs={{0,1},{1,0},{2,3},{3,2},{4,5},{5,4},{6,7},{7,6},{8,9},{9,8},{10,11... | collective-permute-start | bytes 36872 | tf_op jit(solution)/shard_map/ppermute | solution.py:19
  237.8 5.1 %collective-permute-start.4 = (f32[3,1024]{1,0:T(4,128)S(1)}, f32[3,1024]{1,0:T(4,128)S(1)}, u32[]{:S(2)}, u32[]{:S(2)}) collective-permute-start(f32[3,1024]{1,0:T(4,128)S(1)} %add_multiply_fusion), channel_id=1, source_target_pairs={{0,2},{1,3},{2,0},{3,1},{4,6},{5,7},{6,4},{7,5},{8,10},{9,11},{10,... | collective-permute-start | bytes 36872 | tf_op jit(solution)/shard_map/ppermute | solution.py:19

commit v3 on v2

--- a/solution.py
+++ b/solution.py
@@ -8,6 +8,7 @@
 from jax.experimental import pallas as pl
 from jax.experimental.pallas import tpu as pltpu
 from jax.sharding import PartitionSpec as P
+
 
 NBINS = 1024
 
@@ -301,8 +302,9 @@
 
 
 def row_kernel(
-    map_ref, mask_ref, turn_ref, high_ref, low_ref, first_ref, second_ref, mid_ref
+    map_ref, mask_ref, turn_ref, high_ref, low_ref, *refs
 ):
+    out_refs, mid_ref = refs[:-1], refs[-1]
     block = map_ref.shape[1]
     left = lax.broadcasted_iota(jnp.int32, (block // 2, LANES), 1) < HALF
 
@@ -335,27 +337,31 @@
             top, low = value[: block // 2, lanes], value[block // 2 :, lanes]
             subs.append(jnp.where(left, top, pltpu.roll(low, HALF, 1)))
             subs.append(jnp.where(left, pltpu.roll(top, HALF, 1), low))
-        for index in range(2):
-            first_ref[k, index] = subs[index]
-            second_ref[k, index] = subs[2 + index]
+        for out_ref, value in zip(out_refs, subs):
+            out_ref[k] = value
         return carry
 
     lax.fori_loop(0, OUTER // 2, family, 0)
 
 
-def bins_kernel(info_ref, bins_ref, flip_ref, out_ref, turn_ref):
+def bins_kernel(info_ref, flip_ref, *refs):
+    bins_refs, out_ref, turn_ref = refs[:-2], refs[-2], refs[-1]
     step = pl.program_id(0)
-    sub = bins_ref.shape[1]
+    sub = bins_refs[0].shape[1]
     parity = info_ref[0]
     upper = info_ref[1]
     dests = out_ref.shape[0]
     width = out_ref.shape[3]
     zero = parity == 0
     high_side = upper == 1
+    flat_refs = [ref.reshape(LANES * sub, LANES) for ref in bins_refs]
     for c in range(sub):
         kappa = step * sub + c
         mirrored = (OUTER - kappa) % OUTER
-        turn_ref[c % 2] = bins_ref[:, c, :].astype(jnp.float32).T
+        for part, ref in enumerate(flat_refs):
+            turn_ref[c % 2, part * LANES : (part + 1) * LANES] = (
+                ref[pl.ds(c, LANES, stride=sub), :].astype(jnp.float32).T
+            )
 
         def column(at):
             return turn_ref[c % 2, pl.ds(at, width, stride=OUTER), :]
@@ -381,17 +387,17 @@
 
 
 def band_kernel(
-    extent, with_edge, info_ref, x_ref, bins0_ref, bins1_ref, turn_ref, high_ref, low_ref,
+    extent, half_chunk, with_edge, info_ref, x_ref, bins0_ref, bins1_ref, turn_ref, high_ref, low_ref,
     fx_ref, *refs,
 ):
     if with_edge:
         sums_ref, edge_ref, mid_ref, power_ref, part_ref = refs
     else:
         sums_ref, mid_ref, power_ref, part_ref = refs
-    sub = pl.program_id(0)
+    sub = half_chunk
     offset = info_ref[0]
     flipped = info_ref[1]
-    hollow = (info_ref[2] == 1) & (sub == 0)
+    hollow = (info_ref[2] == 1) if sub == 0 else False
     per_slab = x_ref.shape[3] // HALF
     even8 = lax.broadcasted_iota(jnp.int32, (8, LANES), 1) % HALF < SUB
 
@@ -424,7 +430,7 @@
     fx = fx_ref[0]
     lane = lax.broadcasted_iota(jnp.int32, (SUB, LANES), 1)
     slot = lax.broadcasted_iota(jnp.int32, (SUB, LANES), 0)
-    keep = jnp.where((slot == 0) & hollow, 0.0, 1.0)
+    keep = jnp.where((slot == 0) & hollow, 0.0, 1.0) if sub == 0 else 1.0
     inv_area = 1.0 / (extent * extent)
     group_iota = lax.broadcasted_iota(jnp.int32, (GROUPS, LANES), 0).astype(jnp.float32).astype(jnp.bfloat16)
     low_iota = lax.broadcasted_iota(jnp.int32, (LOWS, LANES), 0).astype(jnp.float32).astype(jnp.bfloat16)
@@ -482,7 +488,7 @@
                 ((bins0_ref, begin0, near), (bins1_ref, begin1, near + 1))
             ):
                 for source in range(count):
-                    at = jnp.minimum(begin + source, bins_ref.shape[0] - 1)
+                    at = min(begin + source, bins_ref.shape[0] - 1)
                     value = bins_ref[at, 0, k]
                     high = jnp.floor(value * (1.0 / LOWS))
                     rows = slice(source * width, (source + 1) * width)
@@ -566,14 +572,18 @@
         grid=(OUTER // sub,),
         in_specs=[
             pl.BlockSpec(memory_space=pltpu.SMEM),
-            pl.BlockSpec((LANES, sub, columns), lambda i: (0, i, 0)),
             pl.BlockSpec((2, 2 * LANES, LANES), lambda i: (0, 0, 0)),
+        ]
+        + [
+            pl.BlockSpec((LANES, sub, LANES), lambda i, part=part: (0, i, part))
+            for part in range(columns // LANES)
         ],
         out_specs=pl.BlockSpec((slabs, 2, OUTER, width, LANES), lambda i: (0, 0, 0, 0, 0)),
         out_shape=jax.ShapeDtypeStruct((slabs, 2, OUTER, width, LANES), jnp.float32),
         scratch_shapes=[pltpu.VMEM((2, columns, LANES), jnp.float32)],
+        cost_estimate=pl.CostEstimate(flops=5 * 10**9, transcendentals=0, bytes_accessed=12 * 2**20),
         name="bins_prep",
-    )(info, bins.reshape(LANES, OUTER, columns), jnp.asarray(flips, jnp.bfloat16))
+    )(info, jnp.asarray(flips, jnp.bfloat16), *[bins.reshape(LANES, OUTER, columns)] * (columns // LANES))
     got_bins = lax.all_to_all(sent_bins, "rows", split_axis=0, concat_axis=0, tiled=True)
 
     block = min(LANES, count)
@@ -581,8 +591,8 @@
     angles = 2 * np.pi * (k1 * np.arange(LANES)[None, :] % extent) / extent
     turns = jnp.asarray(np.stack([np.cos(angles), -np.sin(angles)]), jnp.float32)
     table_spec = pl.BlockSpec((2, 2 * LANES, 2 * LANES), lambda i: (0, 0, 0))
-    piece = jax.ShapeDtypeStruct((2 * slabs, 2, count // 2, LANES), jnp.float32)
-    piece_spec = pl.BlockSpec((2 * slabs, 2, block // 2, LANES), lambda i: (0, 0, i, 0))
+    piece = jax.ShapeDtypeStruct((2 * slabs, count // 2, LANES), jnp.float32)
+    piece_spec = pl.BlockSpec((2 * slabs, block // 2, LANES), lambda i: (0, i, 0))
     pieces = pl.pallas_call(
         row_kernel,
         grid=(count // block,),
@@ -593,9 +603,10 @@
             table_spec,
             table_spec,
         ],
-        out_specs=[piece_spec, piece_spec],
-        out_shape=[piece, piece],
+        out_specs=[piece_spec] * (LANES // SUB),
+        out_shape=[piece] * (LANES // SUB),
         scratch_shapes=[pltpu.VMEM((OUTER // 2, block, 2 * LANES), jnp.float32)],
+        cost_estimate=pl.CostEstimate(flops=12 * 10**9, transcendentals=0, bytes_accessed=24 * 2**20),
         name="row_fft",
     )(maps, mask, turns, row_high, row_low)
 
@@ -610,25 +621,33 @@
     slots = lax.iota(jnp.int32, HALF)
     zero = (fam == 0).astype(jnp.int32)
     total = None
-    for chunk, piece in enumerate(pieces):
+    before = got_bins
+    for number, piece in enumerate(pieces):
+        chunk, half_chunk = number // 2, number % 2
+        piece, before = lax.optimization_barrier((piece, before))
         got = lax.all_to_all(
             piece, ("rows", "rep"), split_axis=0, concat_axis=0, tiled=True,
             axis_index_groups=groups,
-        ).reshape(slabs, 2, -1, count // 2, LANES)
+        )
+        before = got
+        got = got.reshape(slabs, 2, -1, count // 2, LANES)
         subs = got.shape[2]
         first_col = OUTER * slots if chunk == 0 else OUTER // 2 + OUTER * (HALF - 1 - slots)
         col = jnp.where(fam == 0, first_col, fam + OUTER * (slots + HALF * chunk))
+        col = col[half_chunk * SUB : (half_chunk + 1) * SUB]
         fx = jnp.broadcast_to(signed_float(col, extent).reshape(subs, SUB, 1), (subs, SUB, LANES))
-        with_edge = chunk == 0
-        if with_edge:
+        with_edge = number == 0
+        if chunk == 0:
             info = jnp.stack([HALF - 1 + zero, jnp.int32(1), zero])
         else:
             info = jnp.stack([jnp.int32(HALF - 1), 1 - zero, jnp.int32(0)])
+        if number == 1:
+            info, special = lax.optimization_barrier((info, special))
         bin_block = (half_slabs, 1, OUTER, width, LANES)
         edge_shape = (subs, OUTER, 2, 2 * LANES)
         sums_shape = (subs, 3 * GROUPS, LOWS)
-        out = pl.pallas_call(
-            functools.partial(band_kernel, extent, with_edge),
+        band_call = pl.pallas_call(
+            functools.partial(band_kernel, extent, half_chunk, with_edge),
             grid=(subs,),
             in_specs=[
                 pl.BlockSpec(memory_space=pltpu.SMEM),
@@ -650,8 +669,10 @@
                 pltpu.VMEM((2, 2, 2, SUB + width, LANES), jnp.float32),
             ],
             compiler_params=pltpu.CompilerParams(vmem_limit_bytes=48 * 2**20),
+            cost_estimate=pl.CostEstimate(flops=10**10, transcendentals=0, bytes_accessed=4 * 2**20),
             name="band_sums",
-        )(info, got, got_bins, got_bins, spin, col_high, col_low, fx)
+        )
+        out = band_call(info, got, got_bins, got_bins, spin, col_high, col_low, fx)
         sums = out[0].sum(0)
         total = sums if total is None else total + sums
         if with_edge:

time: 244 us -> 248 us (1.016)
  waiting for transfers between devices: 87.3 us -> 56.3 us
  blocking collectives: 0 us -> 30.2 us
  Pallas kernels: 119 us -> 122 us
    all_to_all x2 -> x3, waiting for transfers between devices: 55.5 us -> 24.7 us  [on_device_fast(): lax.all_to_all(piece, ('rows', 'rep'), split_axis=0, concat_axis=0, tiled...]
    all_to_all x0 -> x1, blocking collectives: none -> 30.2 us  [on_device_fast(): lax.all_to_all(piece, ('rows', 'rep'), split_axis=0, concat_axis=0, tiled...]
    pallas_call x2 -> x4, Pallas kernels: 81.1 us -> 83.8 us  [on_device_fast(): out = band_call(info, got, got_bins, got_bins, spin, col_high, col_low, fx)]
    unnamed x18 -> x20, local copies, waits for them, and re-layouts: 3.64 us -> 5.21 us
    all_to_all x2 -> x3, starting transfers between devices: 11.5 us -> 13 us  [on_device_fast(): lax.all_to_all(piece, ('rows', 'rep'), split_axis=0, concat_axis=0, tiled...]
  transfers between devices with their start and end apart: 8 -> 9, of which waited for: 8 -> 8; matrix products, arithmetic and copies ran while one was open for 4% -> 4% of each run, Pallas kernels for 28% -> 36%
where the time goes in v3:
time: 248 us
  Pallas kernels  122 us (49%)
  waiting for transfers between devices  56.3 us (23%)
  blocking collectives  30.2 us (12%)
  starting transfers between devices  26.1 us (11%)
  local copies, waits for them, and re-layouts  8.76 us (4%)
  other arithmetic  3.66 us (1%)
    pallas_call x4, Pallas kernels, on_device_fast(): out = band_call(info, got, got_bins, got_bins, spin, col_high, col_low, fx)  83.8 us
    all_to_all x1, blocking collectives, on_device_fast(): lax.all_to_all(piece, ('rows', 'rep'), split_axis=0, concat_axis=0, tiled...  30.2 us
    pallas_call x1, Pallas kernels, on_device_fast(): pl.pallas_call(row_kernel, grid=(count // block,), in_specs=[pl.BlockSpec...  27 us
    all_to_all x3, waiting for transfers between devices, on_device_fast(): lax.all_to_all(piece, ('rows', 'rep'), split_axis=0, concat_axis=0, tiled...  24.7 us
    all_to_all x1, waiting for transfers between devices, on_device_fast(): lax.all_to_all(sent_bins, 'rows', split_axis=0, concat_axis=0, tiled=True)  22.2 us
    all_to_all x3, starting transfers between devices, on_device_fast(): lax.all_to_all(piece, ('rows', 'rep'), split_axis=0, concat_axis=0, tiled...  13 us
    pallas_call x1, Pallas kernels, on_device_fast(): pl.pallas_call(bins_kernel, grid=(OUTER // sub,), in_specs=[pl.BlockSpec(...  11.2 us
    ppermute x5, waiting for transfers between devices, partner(): lax.ppermute(array, axis, [(i, i ^ 1 << distance) for i in range(lax.axis...  9.41 us
  transfers between devices with their start and end apart: 9, of which 8 were waited for; matrix products, arithmetic and copies ran while one was open for 4% of the time, Pallas kernels for 36%

profile of v3, /device:TPU:0, one launch (start us, length us, event | category | flops | bytes accessed | tf_op | source)
XLA Modules:
  0.0 247.8 jit_solution(1960877301530150952)
XLA Ops:
  0.6 11.2 %bins_prep.1 = f32[8,2,32,16,128]{4,3,2,1,0:T(8,128)} custom-call(s32[2]{0:T(128)} %pad_add_fusion.1.info_ref, bf16[2,256,128]{2,1,0:T(8,128)(2,1)} %constant.112.clone.flip_ref, s32[128,32,512]{2,1,0:T(8,128)} %bitcast.35, s32[128,32,512]{2,1,0:T(8,128)} %bitcast.36, s32[128,32,512]{2,1,0:T(8,128)} %bitcast.37, s32[128,32,512]{2,1,0:T(8,128)} %bitcast.38), custom_call_target="tpu_custom_call" | custom-call | flops 5000000000 | bytes 12582912 | tf_op jit(solution)/shard_map/bins_prep/pallas_call | solution.py:570
  11.8 5.2 %all-to-all-start = ((f32[8,2,32,16,128]{4,3,2,1,0:T(8,128)}), f32[8,2,32,16,128]{4,3,2,1,0:T(8,128)}, u32[]{:S(2)}, u32[]{:S(2)}) async-start(f32[8,2,32,16,128]{4,3,2,1,0:T(8,128)} %bins_prep.1), calls=%async_computation | async-start | bytes 8388608 | tf_op jit(solution)/shard_map/all_to_all | solution.py:587
  17.0 27.0 %row_fft.1 = (f32[16,256,128]{2,1,0:T(8,128)}, f32[16,256,128]{2,1,0:T(8,128)}, f32[16,256,128]{2,1,0:T(8,128)}, f32[16,256,128]{2,1,0:T(8,128)}) custom-call(f32[1,512,4096]{2,1,0:T(8,128)} %map_ref.1, s32[512,4096]{1,0:T(8,128)} %mask_ref.1, f32[2,16,128]{2,1,0:T(8,128)} %constant.113.clone.turn_ref, bf16[2,256,256]{2,1,0:T(8,128)(2,1)} %constant.118.high_ref, ...), custom_call_target="tpu_custom_call" | custom-call | flops 12000000000 | bytes 25165824 | tf_op jit(solution)/shard_map/row_fft/pallas_call | solution.py:596
  44.0 22.2 %all-to-all-done.bins0_ref.bins1_ref = f32[8,2,32,16,128]{4,3,2,1,0:T(8,128)} async-done(((f32[8,2,32,16,128]{4,3,2,1,0:T(8,128)}), f32[8,2,32,16,128]{4,3,2,1,0:T(8,128)}, u32[]{:S(2)}, u32[]{:S(2)}) %all-to-all-start) | async-done | bytes 4194336 | tf_op jit(solution)/shard_map/all_to_all | solution.py:587
  66.2 30.2 %all_to_all.25 = f32[16,256,128]{2,1,0:T(8,128)} all-to-all(f32[16,256,128]{2,1,0:T(8,128)} %get-tuple-element.18), channel_id=1, replica_groups={{0,1,4,5,8,9,12,13,16,17,20,21,24,25,28,29},{2,3,6,7,10,11,14,15,18,19,..., dimensions={0} | all-to-all | bytes 4194304 | tf_op jit(solution)/shard_map/all_to_all | solution.py:628
  96.4 3.7 %all-to-all-start.2 = ((f32[16,256,128]{2,1,0:T(8,128)}), f32[16,256,128]{2,1,0:T(8,128)S(1)}, u32[]{:S(2)}, u32[]{:S(2)}) async-start(f32[16,256,128]{2,1,0:T(8,128)} %get-tuple-element.23), calls=%async_computation.2 | async-start | bytes 4194304 | tf_op jit(solution)/shard_map/all_to_all | solution.py:628
  103.9 23.5 %all-to-all-done.2 = f32[16,256,128]{2,1,0:T(8,128)S(1)} async-done(((f32[16,256,128]{2,1,0:T(8,128)}), f32[16,256,128]{2,1,0:T(8,128)S(1)}, u32[]{:S(2)}, u32[]{:S(2)}) %all-to-all-start.2) | async-done | bytes 2097184 | tf_op jit(solution)/shard_map/all_to_all | solution.py:628
  127.4 4.7 %all-to-all-start.3 = ((f32[16,256,128]{2,1,0:T(8,128)}), f32[16,256,128]{2,1,0:T(8,128)}, u32[]{:S(2)}, u32[]{:S(2)}) async-start(f32[16,256,128]{2,1,0:T(8,128)} %get-tuple-element.25), calls=%async_computation.3 | async-start | bytes 4194304 | tf_op jit(solution)/shard_map/all_to_all | solution.py:628
  132.2 1.6 copy-done
  133.8 20.7 %band_sums.4 = (f32[1,48,64]{2,1,0:T(8,128)S(1)}, f32[1,32,2,256]{3,2,1,0:T(2,128)S(1)}) custom-call(s32[3]{0:T(128)S(1)} %pad_add_fusion.info_ref, f32[8,2,1,256,128]{4,3,2,1,0:T(8,128)S(1)} %bitcast.33, f32[8,2,32,16,128]{4,3,2,1,0:T(8,128)} %all-to-all-done.bins0_ref.bins1_ref, f32[8,2,32,16,128]{4,3,2,1,0:T(8,128)} %all-to-all-done.bins0_ref.bins1_ref, ...), custom_call_target="tpu_custom_call" | custom-call | flops 10000000000 | bytes 4194304 | tf_op jit(solution)/shard_map/band_sums/pallas_call | solution.py:675
  154.9 2.9 %reverse.5 = f32[2,2,4096]{2,1,0:T(2,128)S(1)} reverse(f32[2,2,4096]{2,1,0:T(2,128)S(1)} %bitcast.41), dimensions={2} | reverse | bytes 131072
  159.8 4.6 %all-to-all-start.4 = ((f32[16,256,128]{2,1,0:T(8,128)}), f32[16,256,128]{2,1,0:T(8,128)}, u32[]{:S(2)}, u32[]{:S(2)}) async-start(f32[16,256,128]{2,1,0:T(8,128)} %get-tuple-element.27), calls=%async_computation.4 | async-start | bytes 4194304 | tf_op jit(solution)/shard_map/all_to_all | solution.py:628
  166.3 20.6 %band_sums.5 = f32[1,48,64]{2,1,0:T(8,128)S(1)} custom-call(s32[3]{0:T(128)S(1)} %pad_add_fusion.info_ref, f32[8,2,1,256,128]{4,3,2,1,0:T(8,128)S(1)} %bitcast.32, f32[8,2,32,16,128]{4,3,2,1,0:T(8,128)} %all-to-all-done.bins0_ref.bins1_ref, f32[8,2,32,16,128]{4,3,2,1,0:T(8,128)} %all-to-all-done.bins0_ref.bins1_ref, f32[2,64,128]{2,1,0:T(8,128)S(1)} %copy-done.3, ...), custom_call_target="tpu_custom_call" | custom-call | flops 10000000000 | bytes 4194304 | tf_op jit(solution)/shard_map/band_sums/pallas_call | solution.py:675
  187.0 21.3 %band_sums.6 = f32[1,48,64]{2,1,0:T(8,128)S(1)} custom-call(s32[3]{0:T(128)S(1)} %pad_add_fusion.2.info_ref, f32[8,2,1,256,128]{4,3,2,1,0:T(8,128)} %bitcast.17.x_ref, f32[8,2,32,16,128]{4,3,2,1,0:T(8,128)} %all-to-all-done.bins0_ref.bins1_ref, f32[8,2,32,16,128]{4,3,2,1,0:T(8,128)} %all-to-all-done.bins0_ref.bins1_ref, f32[2,64,128]{2,1,0:T(8,128)S(1)} %copy-done.3, ...), custom_call_target="tpu_custom_call" | custom-call | flops 10000000000 | bytes 4194304 | tf_op jit(solution)/shard_map/band_sums/pallas_call | solution.py:675
  208.4 21.2 %band_sums.7 = f32[1,48,64]{2,1,0:T(8,128)S(1)} custom-call(s32[3]{0:T(128)S(1)} %pad_add_fusion.2.info_ref, f32[8,2,1,256,128]{4,3,2,1,0:T(8,128)} %bitcast.18.x_ref, f32[8,2,32,16,128]{4,3,2,1,0:T(8,128)} %all-to-all-done.bins0_ref.bins1_ref, f32[8,2,32,16,128]{4,3,2,1,0:T(8,128)} %all-to-all-done.bins0_ref.bins1_ref, f32[2,64,128]{2,1,0:T(8,128)S(1)} %copy-done.3, ...), custom_call_target="tpu_custom_call" | custom-call | flops 10000000000 | bytes 4194304 | tf_op jit(solution)/shard_map/band_sums/pallas_call | solution.py:675
  229.8 1.2 collective-permute-done
  231.0 1.6 collective-permute-start.1
  232.5 2.2 collective-permute-done.1
  234.7 1.6 collective-permute-start.2
  236.3 2.2 collective-permute-done.2
  238.5 1.5 collective-permute-start.3
  240.0 2.2 collective-permute-done.3
  242.3 3.2 %collective-permute-start.4 = (f32[3,1024]{1,0:T(4,128)S(1)}, f32[3,1024]{1,0:T(4,128)S(1)}, u32[]{:S(2)}, u32[]{:S(2)}) collective-permute-start(f32[3,1024]{1,0:T(4,128)S(1)} %add_multiply_fusion), channel_id=1, source_target_pairs={{0,2},{1,3},{2,0},{3,1},{4,6},{5,7},{6,4},{7,5},{8,10},{9,11},{10,... | collective-permute-start | bytes 36872 | tf_op jit(solution)/shard_map/ppermute | solution.py:20
  245.5 1.7 collective-permute-done.4
  (69 shorter events, 9.7 us)
Async XLA Ops:
  11.8 54.4 %all-to-all-start = ((f32[8,2,32,16,128]{4,3,2,1,0:T(8,128)}), f32[8,2,32,16,128]{4,3,2,1,0:T(8,128)}, u32[]{:S(2)}, u32[]{:S(2)}) async-start(f32[8,2,32,16,128]{4,3,2,1,0:T(8,128)} %bins_prep.1), calls=%async_computation | async-start | bytes 8388608 | tf_op jit(solution)/shard_map/all_to_all | solution.py:587
  96.4 31.0 %all-to-all-start.2 = ((f32[16,256,128]{2,1,0:T(8,128)}), f32[16,256,128]{2,1,0:T(8,128)S(1)}, u32[]{:S(2)}, u32[]{:S(2)}) async-start(f32[16,256,128]{2,1,0:T(8,128)} %get-tuple-element.23), calls=%async_computation.2 | async-start | bytes 4194304 | tf_op jit(solution)/shard_map/all_to_all | solution.py:628
  127.4 4.7 %copy-start.1 = (bf16[256,256]{1,0:T(8,128)(2,1)S(1)}, bf16[256,256]{1,0:T(8,128)(2,1)}, u32[]{:S(2)}) copy-start(bf16[256,256]{1,0:T(8,128)(2,1)} %constant.122.high_ref) | copy-start | bytes 393220
  127.4 4.7 %copy-start.2 = (bf16[256,256]{1,0:T(8,128)(2,1)S(1)}, bf16[256,256]{1,0:T(8,128)(2,1)}, u32[]{:S(2)}) copy-start(bf16[256,256]{1,0:T(8,128)(2,1)} %constant.125.low_ref) | copy-start | bytes 393220
  127.4 4.7 %copy-start.3 = (f32[2,64,128]{2,1,0:T(8,128)S(1)}, f32[2,64,128]{2,1,0:T(8,128)}, u32[]{:S(2)}) copy-start(f32[2,64,128]{2,1,0:T(8,128)} %constant.114.clone.turn_ref) | copy-start | bytes 196612
  127.4 32.4 %all-to-all-start.3 = ((f32[16,256,128]{2,1,0:T(8,128)}), f32[16,256,128]{2,1,0:T(8,128)}, u32[]{:S(2)}, u32[]{:S(2)}) async-start(f32[16,256,128]{2,1,0:T(8,128)} %get-tuple-element.25), calls=%async_computation.3 | async-start | bytes 4194304 | tf_op jit(solution)/shard_map/all_to_all | solution.py:628
  132.2 1.6 copy-start
  133.8 24.5 %copy-start.4 = (f32[2]{0:T(128)S(1)}, f32[2]{0:T(128)}, u32[]{:S(2)}) copy-start(f32[2]{0:T(128)} %constant.126) | copy-start | bytes 28
  133.8 24.5 %copy-start.5 = (f32[2]{0:T(128)S(1)}, f32[2]{0:T(128)}, u32[]{:S(2)}) copy-start(f32[2]{0:T(128)} %constant.127) | copy-start | bytes 28
  159.8 48.5 %all-to-all-start.4 = ((f32[16,256,128]{2,1,0:T(8,128)}), f32[16,256,128]{2,1,0:T(8,128)}, u32[]{:S(2)}, u32[]{:S(2)}) async-start(f32[16,256,128]{2,1,0:T(8,128)} %get-tuple-element.27), calls=%async_computation.4 | async-start | bytes 4194304 | tf_op jit(solution)/shard_map/all_to_all | solution.py:628
  208.4 33.8 %copy-start.6 = (f32[3]{0:T(128)S(1)}, f32[3]{0:T(128)}, u32[]{:S(2)}) copy-start(f32[3]{0:T(128)} %constant.116.clone) | copy-start | bytes 40
  229.7 1.2 collective-permute-start
  231.0 3.7 %collective-permute-start.1 = (f32[3,1024]{1,0:T(4,128)S(1)}, f32[3,1024]{1,0:T(4,128)S(1)}, u32[]{:S(2)}, u32[]{:S(2)}) collective-permute-start(f32[3,1024]{1,0:T(4,128)S(1)} %add.285), channel_id=1, source_target_pairs={{0,8},{4,12},{8,0},{12,4},{16,24},{20,28},{24,16},{28,20},{1,9},{5... | collective-permute-start | bytes 36872 | tf_op jit(solution)/shard_map/ppermute | solution.py:20
  234.7 3.7 %collective-permute-start.2 = (f32[3,1024]{1,0:T(4,128)S(1)}, f32[3,1024]{1,0:T(4,128)S(1)}, u32[]{:S(2)}, u32[]{:S(2)}) collective-permute-start(f32[3,1024]{1,0:T(4,128)S(1)} %add.286), channel_id=1, source_target_pairs={{0,16},{4,20},{8,24},{12,28},{16,0},{20,4},{24,8},{28,12},{1,17},{... | collective-permute-start | bytes 36872 | tf_op jit(solution)/shard_map/ppermute | solution.py:20
  238.5 3.7 %collective-permute-start.3 = (f32[3,1024]{1,0:T(4,128)S(1)}, f32[3,1024]{1,0:T(4,128)S(1)}, u32[]{:S(2)}, u32[]{:S(2)}) collective-permute-start(f32[3,1024]{1,0:T(4,128)S(1)} %add.287), channel_id=1, source_target_pairs={{0,1},{1,0},{2,3},{3,2},{4,5},{5,4},{6,7},{7,6},{8,9},{9,8},{10,11... | collective-permute-start | bytes 36872 | tf_op jit(solution)/shard_map/ppermute | solution.py:20
  242.3 4.9 %collective-permute-start.4 = (f32[3,1024]{1,0:T(4,128)S(1)}, f32[3,1024]{1,0:T(4,128)S(1)}, u32[]{:S(2)}, u32[]{:S(2)}) collective-permute-start(f32[3,1024]{1,0:T(4,128)S(1)} %add_multiply_fusion), channel_id=1, source_target_pairs={{0,2},{1,3},{2,0},{3,1},{4,6},{5,7},{6,4},{7,5},{8,10},{9,11},{10,... | collective-permute-start | bytes 36872 | tf_op jit(solution)/shard_map/ppermute | solution.py:20

commit v4 on v3

--- a/solution.py
+++ b/solution.py
@@ -198,6 +198,7 @@
 OUTER = 32
 HALF = LANES // 2
 SUB = LANES // 4
+BATCH = 4
 GROUPS = 16
 LOWS = 64
 
@@ -442,15 +443,15 @@
     begin0 = sub * near
     begin1 = (1 - sub) * near
 
-    def pair(step, acc):
+    def batch(step, acc):
         turned_rows = []
-        for member in range(2):
-            flat = mid_ref[2 * step + member].T
+        for member in range(BATCH):
+            flat = mid_ref[BATCH * step + member].T
             turned_rows.append(jnp.concatenate([flat[:HALF], flat[HALF:]], 1))
         spectra = three_pass(jnp.concatenate(turned_rows, 0), high_ref[...], low_ref[...])
         weighted, lows = [], []
-        for member in range(2):
-            k = 2 * step + member
+        for member in range(BATCH):
+            k = BATCH * step + member
             spectrum = spectra[member * HALF : (member + 1) * HALF]
             if with_edge:
                 edge_ref[sub, k, 0:1, :] = spectrum[0:1, :]
@@ -514,7 +515,7 @@
             jnp.concatenate(weighted, 1), jnp.concatenate(lows, 1), (((1,), (1,)), ((), ()))
         )
 
-    sums_ref[0] = lax.fori_loop(0, OUTER // 2, pair, jnp.zeros((3 * GROUPS, LOWS), jnp.float32))
+    sums_ref[0] = lax.fori_loop(0, OUTER // BATCH, batch, jnp.zeros((3 * GROUPS, LOWS), jnp.float32))
 
 
 def summed(array, axis):
@@ -665,8 +666,8 @@
             + [jax.ShapeDtypeStruct(edge_shape, jnp.float32)] * with_edge,
             scratch_shapes=[
                 pltpu.VMEM((OUTER, LANES, LANES), jnp.float32),
-                pltpu.VMEM((2, 2, 3, SUB, LANES), jnp.float32),
-                pltpu.VMEM((2, 2, 2, SUB + width, LANES), jnp.float32),
+                pltpu.VMEM((BATCH, 2, 3, SUB, LANES), jnp.float32),
+                pltpu.VMEM((BATCH, 2, 2, SUB + width, LANES), jnp.float32),
             ],
             compiler_params=pltpu.CompilerParams(vmem_limit_bytes=48 * 2**20),
             cost_estimate=pl.CostEstimate(flops=10**10, transcendentals=0, bytes_accessed=4 * 2**20),
@@ -685,12 +686,15 @@
     cross = math.sqrt(auto)
     factors = jnp.array([auto, auto, cross], jnp.float32)[:, None]
     own = summed(partial_sums, "rows")
-    own = (own + partner(own, "rep", 0)) * factors
-    skies = [own]
-    distance = 1
-    while 1 << distance < reps:
-        skies = skies + [partner(sky, "rep", distance) for sky in skies]
-        distance += 1
+
+    def from_rep(shift):
+        if shift == 0:
+            return own
+        return lax.ppermute(own, "rep", [(i, i ^ shift) for i in range(reps)])
+
+    skies = [
+        (from_rep(2 * shift) + from_rep(2 * shift + 1)) * factors for shift in range(reps // 2)
+    ]
     stacked = jnp.stack(skies)
     order = lax.iota(jnp.int32, len(skies)) ^ (member // 2)
     return jnp.take(stacked, order, axis=0) if len(skies) > 2 else jnp.where(

time: 248 us -> 242 us (0.976)
  Pallas kernels: 122 us -> 111 us
  waiting for transfers between devices: 56.3 us -> 60.8 us
    pallas_call x4, Pallas kernels: 83.8 us -> 72.4 us  [on_device_fast(): out = band_call(info, got, got_bins, got_bins, spin, col_high, col_low, fx)]
    ppermute x0 -> x3, waiting for transfers between devices: none -> 5.53 us  [from_rep(): return lax.ppermute(own, 'rep', [(i, i ^ shift) for i in range(reps)])]
    ppermute x0 -> x3, starting transfers between devices: none -> 4.74 us  [from_rep(): return lax.ppermute(own, 'rep', [(i, i ^ shift) for i in range(reps)])]
    ppermute x5 -> x3, starting transfers between devices: 7.95 us -> 3.27 us  [partner(): lax.ppermute(array, axis, [(i, i ^ 1 << distance) for i in range(lax.axis...]
    ppermute x5 -> x3, waiting for transfers between devices: 9.41 us -> 5.45 us  [partner(): lax.ppermute(array, axis, [(i, i ^ 1 << distance) for i in range(lax.axis...]
    all_to_all x3, waiting for transfers between devices: 24.7 us -> 27.6 us  [on_device_fast(): lax.all_to_all(piece, ('rows', 'rep'), split_axis=0, concat_axis=0, tiled...]
  transfers between devices with their start and end apart: 9 -> 10, of which waited for: 8 -> 8; matrix products, arithmetic and copies ran while one was open for 4% -> 4% of each run, Pallas kernels for 36% -> 34%
where the time goes in v4:
time: 242 us; the launch traced here: 241 us
  Pallas kernels  111 us (46%)
  waiting for transfers between devices  60.8 us (25%)
  blocking collectives  30.2 us (12%)
  starting transfers between devices  26.2 us (11%)
  local copies, waits for them, and re-layouts  8.76 us (4%)
  other arithmetic  3.73 us (2%)
    pallas_call x4, Pallas kernels, on_device_fast(): out = band_call(info, got, got_bins, got_bins, spin, col_high, col_low, fx)  72.4 us
    all_to_all x1, blocking collectives, on_device_fast(): lax.all_to_all(piece, ('rows', 'rep'), split_axis=0, concat_axis=0, tiled...  30.2 us
    all_to_all x3, waiting for transfers between devices, on_device_fast(): lax.all_to_all(piece, ('rows', 'rep'), split_axis=0, concat_axis=0, tiled...  27.6 us
    pallas_call x1, Pallas kernels, on_device_fast(): pl.pallas_call(row_kernel, grid=(count // block,), in_specs=[pl.BlockSpec...  27 us
    all_to_all x1, waiting for transfers between devices, on_device_fast(): lax.all_to_all(sent_bins, 'rows', split_axis=0, concat_axis=0, tiled=True)  22.2 us
    all_to_all x3, starting transfers between devices, on_device_fast(): lax.all_to_all(piece, ('rows', 'rep'), split_axis=0, concat_axis=0, tiled...  13 us
    pallas_call x1, Pallas kernels, on_device_fast(): pl.pallas_call(bins_kernel, grid=(OUTER // sub,), in_specs=[pl.BlockSpec(...  11.2 us
    ppermute x3, waiting for transfers between devices, from_rep(): return lax.ppermute(own, 'rep', [(i, i ^ shift) for i in range(reps)])  5.53 us
  transfers between devices with their start and end apart: 10, of which 8 were waited for; matrix products, arithmetic and copies ran while one was open for 4% of the time, Pallas kernels for 34%

profile of v4, /device:TPU:0, one launch (start us, length us, event | category | flops | bytes accessed | tf_op | source)
XLA Modules:
  0.0 241.0 jit_solution(14153945984434925457)
XLA Ops:
  0.7 11.2 %bins_prep.1 = f32[8,2,32,16,128]{4,3,2,1,0:T(8,128)} custom-call(s32[2]{0:T(128)} %pad_add_fusion.1.info_ref, bf16[2,256,128]{2,1,0:T(8,128)(2,1)} %constant.112.clone.flip_ref, s32[128,32,512]{2,1,0:T(8,128)} %bitcast.37, s32[128,32,512]{2,1,0:T(8,128)} %bitcast.38, s32[128,32,512]{2,1,0:T(8,128)} %bitcast.39, s32[128,32,512]{2,1,0:T(8,128)} %bitcast.40), custom_call_target="tpu_custom_call" | custom-call | flops 5000000000 | bytes 12582912 | tf_op jit(solution)/shard_map/bins_prep/pallas_call | solution.py:571
  11.8 5.2 %all-to-all-start = ((f32[8,2,32,16,128]{4,3,2,1,0:T(8,128)}), f32[8,2,32,16,128]{4,3,2,1,0:T(8,128)}, u32[]{:S(2)}, u32[]{:S(2)}) async-start(f32[8,2,32,16,128]{4,3,2,1,0:T(8,128)} %bins_prep.1), calls=%async_computation | async-start | bytes 8388608 | tf_op jit(solution)/shard_map/all_to_all | solution.py:588
  17.0 27.0 %row_fft.1 = (f32[16,256,128]{2,1,0:T(8,128)}, f32[16,256,128]{2,1,0:T(8,128)}, f32[16,256,128]{2,1,0:T(8,128)}, f32[16,256,128]{2,1,0:T(8,128)}) custom-call(f32[1,512,4096]{2,1,0:T(8,128)} %map_ref.1, s32[512,4096]{1,0:T(8,128)} %mask_ref.1, f32[2,16,128]{2,1,0:T(8,128)} %constant.113.clone.turn_ref, bf16[2,256,256]{2,1,0:T(8,128)(2,1)} %constant.118.high_ref, ...), custom_call_target="tpu_custom_call" | custom-call | flops 12000000000 | bytes 25165824 | tf_op jit(solution)/shard_map/row_fft/pallas_call | solution.py:597
  44.0 22.2 %all-to-all-done.bins0_ref.bins1_ref = f32[8,2,32,16,128]{4,3,2,1,0:T(8,128)} async-done(((f32[8,2,32,16,128]{4,3,2,1,0:T(8,128)}), f32[8,2,32,16,128]{4,3,2,1,0:T(8,128)}, u32[]{:S(2)}, u32[]{:S(2)}) %all-to-all-start) | async-done | bytes 4194336 | tf_op jit(solution)/shard_map/all_to_all | solution.py:588
  66.2 30.2 %all_to_all.25 = f32[16,256,128]{2,1,0:T(8,128)} all-to-all(f32[16,256,128]{2,1,0:T(8,128)} %get-tuple-element.18), channel_id=1, replica_groups={{0,1,4,5,8,9,12,13,16,17,20,21,24,25,28,29},{2,3,6,7,10,11,14,15,18,19,..., dimensions={0} | all-to-all | bytes 4194304 | tf_op jit(solution)/shard_map/all_to_all | solution.py:629
  96.4 3.7 %all-to-all-start.2 = ((f32[16,256,128]{2,1,0:T(8,128)}), f32[16,256,128]{2,1,0:T(8,128)S(1)}, u32[]{:S(2)}, u32[]{:S(2)}) async-start(f32[16,256,128]{2,1,0:T(8,128)} %get-tuple-element.23), calls=%async_computation.2 | async-start | bytes 4194304 | tf_op jit(solution)/shard_map/all_to_all | solution.py:629
  104.0 23.5 %all-to-all-done.2 = f32[16,256,128]{2,1,0:T(8,128)S(1)} async-done(((f32[16,256,128]{2,1,0:T(8,128)}), f32[16,256,128]{2,1,0:T(8,128)S(1)}, u32[]{:S(2)}, u32[]{:S(2)}) %all-to-all-start.2) | async-done | bytes 2097184 | tf_op jit(solution)/shard_map/all_to_all | solution.py:629
  127.5 4.7 %all-to-all-start.3 = ((f32[16,256,128]{2,1,0:T(8,128)}), f32[16,256,128]{2,1,0:T(8,128)}, u32[]{:S(2)}, u32[]{:S(2)}) async-start(f32[16,256,128]{2,1,0:T(8,128)} %get-tuple-element.25), calls=%async_computation.3 | async-start | bytes 4194304 | tf_op jit(solution)/shard_map/all_to_all | solution.py:629
  132.2 1.6 copy-done
  133.8 17.8 %band_sums.4 = (f32[1,48,64]{2,1,0:T(8,128)S(1)}, f32[1,32,2,256]{3,2,1,0:T(2,128)S(1)}) custom-call(s32[3]{0:T(128)S(1)} %pad_add_fusion.info_ref, f32[8,2,1,256,128]{4,3,2,1,0:T(8,128)S(1)} %bitcast.35, f32[8,2,32,16,128]{4,3,2,1,0:T(8,128)} %all-to-all-done.bins0_ref.bins1_ref, f32[8,2,32,16,128]{4,3,2,1,0:T(8,128)} %all-to-all-done.bins0_ref.bins1_ref, ...), custom_call_target="tpu_custom_call" | custom-call | flops 10000000000 | bytes 4194304 | tf_op jit(solution)/shard_map/band_sums/pallas_call | solution.py:676
  152.1 2.9 %reverse.5 = f32[2,2,4096]{2,1,0:T(2,128)S(1)} reverse(f32[2,2,4096]{2,1,0:T(2,128)S(1)} %bitcast.43), dimensions={2} | reverse | bytes 131072
  155.8 4.0 %all-to-all-done.3 = f32[16,256,128]{2,1,0:T(8,128)} async-done(((f32[16,256,128]{2,1,0:T(8,128)}), f32[16,256,128]{2,1,0:T(8,128)}, u32[]{:S(2)}, u32[]{:S(2)}) %all-to-all-start.3) | async-done | bytes 2097184 | tf_op jit(solution)/shard_map/all_to_all | solution.py:629
  159.9 4.6 %all-to-all-start.4 = ((f32[16,256,128]{2,1,0:T(8,128)}), f32[16,256,128]{2,1,0:T(8,128)}, u32[]{:S(2)}, u32[]{:S(2)}) async-start(f32[16,256,128]{2,1,0:T(8,128)} %get-tuple-element.27), calls=%async_computation.4 | async-start | bytes 4194304 | tf_op jit(solution)/shard_map/all_to_all | solution.py:629
  166.3 17.8 %band_sums.5 = f32[1,48,64]{2,1,0:T(8,128)S(1)} custom-call(s32[3]{0:T(128)S(1)} %pad_add_fusion.info_ref, f32[8,2,1,256,128]{4,3,2,1,0:T(8,128)S(1)} %bitcast.34, f32[8,2,32,16,128]{4,3,2,1,0:T(8,128)} %all-to-all-done.bins0_ref.bins1_ref, f32[8,2,32,16,128]{4,3,2,1,0:T(8,128)} %all-to-all-done.bins0_ref.bins1_ref, f32[2,64,128]{2,1,0:T(8,128)S(1)} %copy-done.3, ...), custom_call_target="tpu_custom_call" | custom-call | flops 10000000000 | bytes 4194304 | tf_op jit(solution)/shard_map/band_sums/pallas_call | solution.py:676
  184.2 18.4 %band_sums.6 = f32[1,48,64]{2,1,0:T(8,128)S(1)} custom-call(s32[3]{0:T(128)S(1)} %pad_add_fusion.2.info_ref, f32[8,2,1,256,128]{4,3,2,1,0:T(8,128)} %bitcast.17.x_ref, f32[8,2,32,16,128]{4,3,2,1,0:T(8,128)} %all-to-all-done.bins0_ref.bins1_ref, f32[8,2,32,16,128]{4,3,2,1,0:T(8,128)} %all-to-all-done.bins0_ref.bins1_ref, f32[2,64,128]{2,1,0:T(8,128)S(1)} %copy-done.3, ...), custom_call_target="tpu_custom_call" | custom-call | flops 10000000000 | bytes 4194304 | tf_op jit(solution)/shard_map/band_sums/pallas_call | solution.py:676
  202.7 18.4 %band_sums.7 = f32[1,48,64]{2,1,0:T(8,128)S(1)} custom-call(s32[3]{0:T(128)S(1)} %pad_add_fusion.2.info_ref, f32[8,2,1,256,128]{4,3,2,1,0:T(8,128)} %bitcast.18.x_ref, f32[8,2,32,16,128]{4,3,2,1,0:T(8,128)} %all-to-all-done.bins0_ref.bins1_ref, f32[8,2,32,16,128]{4,3,2,1,0:T(8,128)} %all-to-all-done.bins0_ref.bins1_ref, f32[2,64,128]{2,1,0:T(8,128)S(1)} %copy-done.3, ...), custom_call_target="tpu_custom_call" | custom-call | flops 10000000000 | bytes 4194304 | tf_op jit(solution)/shard_map/band_sums/pallas_call | solution.py:676
  222.5 1.6 collective-permute-start.1
  224.1 2.2 collective-permute-done.1
  226.2 1.6 collective-permute-start.2
  227.8 2.1 collective-permute-done.2
  230.0 1.6 collective-permute-start.3
  231.5 3.2 %collective-permute-start.4 = (f32[3,1024]{1,0:T(4,128)S(1)}, f32[3,1024]{1,0:T(4,128)S(1)}, u32[]{:S(2)}, u32[]{:S(2)}) collective-permute-start(f32[3,1024]{1,0:T(4,128)S(1)} %add.290), channel_id=1, source_target_pairs={{0,2},{1,3},{2,0},{3,1},{4,6},{5,7},{6,4},{7,5},{8,10},{9,11},{10,... | collective-permute-start | bytes 36872 | tf_op jit(solution)/shard_map/ppermute | solution.py:693
  234.7 1.7 collective-permute-done.4
  236.4 3.8 %collective-permute-done.5 = f32[3,1024]{1,0:T(4,128)S(1)} collective-permute-done((f32[3,1024]{1,0:T(4,128)S(1)}, f32[3,1024]{1,0:T(4,128)S(1)}, u32[]{:S(2)}, u32[]{:S(2)}) %collective-permute-start.5) | collective-permute-done | bytes 12320 | tf_op jit(solution)/shard_map/ppermute | solution.py:693
  (71 shorter events, 9.8 us)
Async XLA Ops:
  11.8 54.4 %all-to-all-start = ((f32[8,2,32,16,128]{4,3,2,1,0:T(8,128)}), f32[8,2,32,16,128]{4,3,2,1,0:T(8,128)}, u32[]{:S(2)}, u32[]{:S(2)}) async-start(f32[8,2,32,16,128]{4,3,2,1,0:T(8,128)} %bins_prep.1), calls=%async_computation | async-start | bytes 8388608 | tf_op jit(solution)/shard_map/all_to_all | solution.py:588
  96.4 31.0 %all-to-all-start.2 = ((f32[16,256,128]{2,1,0:T(8,128)}), f32[16,256,128]{2,1,0:T(8,128)S(1)}, u32[]{:S(2)}, u32[]{:S(2)}) async-start(f32[16,256,128]{2,1,0:T(8,128)} %get-tuple-element.23), calls=%async_computation.2 | async-start | bytes 4194304 | tf_op jit(solution)/shard_map/all_to_all | solution.py:629
  127.5 4.7 %copy-start.1 = (bf16[256,256]{1,0:T(8,128)(2,1)S(1)}, bf16[256,256]{1,0:T(8,128)(2,1)}, u32[]{:S(2)}) copy-start(bf16[256,256]{1,0:T(8,128)(2,1)} %constant.122.high_ref) | copy-start | bytes 393220
  127.5 4.7 %copy-start.2 = (bf16[256,256]{1,0:T(8,128)(2,1)S(1)}, bf16[256,256]{1,0:T(8,128)(2,1)}, u32[]{:S(2)}) copy-start(bf16[256,256]{1,0:T(8,128)(2,1)} %constant.125.low_ref) | copy-start | bytes 393220
  127.5 4.7 %copy-start.3 = (f32[2,64,128]{2,1,0:T(8,128)S(1)}, f32[2,64,128]{2,1,0:T(8,128)}, u32[]{:S(2)}) copy-start(f32[2,64,128]{2,1,0:T(8,128)} %constant.114.clone.turn_ref) | copy-start | bytes 196612
  127.5 32.4 %all-to-all-start.3 = ((f32[16,256,128]{2,1,0:T(8,128)}), f32[16,256,128]{2,1,0:T(8,128)}, u32[]{:S(2)}, u32[]{:S(2)}) async-start(f32[16,256,128]{2,1,0:T(8,128)} %get-tuple-element.25), calls=%async_computation.3 | async-start | bytes 4194304 | tf_op jit(solution)/shard_map/all_to_all | solution.py:629
  132.2 1.6 copy-start
  133.8 21.6 %copy-start.4 = (f32[2]{0:T(128)S(1)}, f32[2]{0:T(128)}, u32[]{:S(2)}) copy-start(f32[2]{0:T(128)} %constant.126) | copy-start | bytes 28
  133.8 21.6 %copy-start.5 = (f32[2]{0:T(128)S(1)}, f32[2]{0:T(128)}, u32[]{:S(2)}) copy-start(f32[2]{0:T(128)} %constant.127) | copy-start | bytes 28
  159.9 42.7 %all-to-all-start.4 = ((f32[16,256,128]{2,1,0:T(8,128)}), f32[16,256,128]{2,1,0:T(8,128)}, u32[]{:S(2)}, u32[]{:S(2)}) async-start(f32[16,256,128]{2,1,0:T(8,128)} %get-tuple-element.27), calls=%async_computation.4 | async-start | bytes 4194304 | tf_op jit(solution)/shard_map/all_to_all | solution.py:629
  202.7 37.6 %copy-start.6 = (f32[3]{0:T(128)S(1)}, f32[3]{0:T(128)}, u32[]{:S(2)}) copy-start(f32[3]{0:T(128)} %constant.116.clone) | copy-start | bytes 40
  221.2 1.2 collective-permute-start
  222.5 3.7 %collective-permute-start.1 = (f32[3,1024]{1,0:T(4,128)S(1)}, f32[3,1024]{1,0:T(4,128)S(1)}, u32[]{:S(2)}, u32[]{:S(2)}) collective-permute-start(f32[3,1024]{1,0:T(4,128)S(1)} %add.288), channel_id=1, source_target_pairs={{0,8},{4,12},{8,0},{12,4},{16,24},{20,28},{24,16},{28,20},{1,9},{5... | collective-permute-start | bytes 36872 | tf_op jit(solution)/shard_map/ppermute | solution.py:20
  226.2 3.7 %collective-permute-start.2 = (f32[3,1024]{1,0:T(4,128)S(1)}, f32[3,1024]{1,0:T(4,128)S(1)}, u32[]{:S(2)}, u32[]{:S(2)}) collective-permute-start(f32[3,1024]{1,0:T(4,128)S(1)} %add.289), channel_id=1, source_target_pairs={{0,16},{4,20},{8,24},{12,28},{16,0},{20,4},{24,8},{28,12},{1,17},{... | collective-permute-start | bytes 36872 | tf_op jit(solution)/shard_map/ppermute | solution.py:20
  230.0 4.7 %collective-permute-start.3 = (f32[3,1024]{1,0:T(4,128)S(1)}, f32[3,1024]{1,0:T(4,128)S(1)}, u32[]{:S(2)}, u32[]{:S(2)}) collective-permute-start(f32[3,1024]{1,0:T(4,128)S(1)} %add.290), channel_id=1, source_target_pairs={{0,1},{1,0},{2,3},{3,2},{4,5},{5,4},{6,7},{7,6},{8,9},{9,8},{10,11... | collective-permute-start | bytes 36872 | tf_op jit(solution)/shard_map/ppermute | solution.py:693
  231.5 4.9 %collective-permute-start.4 = (f32[3,1024]{1,0:T(4,128)S(1)}, f32[3,1024]{1,0:T(4,128)S(1)}, u32[]{:S(2)}, u32[]{:S(2)}) collective-permute-start(f32[3,1024]{1,0:T(4,128)S(1)} %add.290), channel_id=1, source_target_pairs={{0,2},{1,3},{2,0},{3,1},{4,6},{5,7},{6,4},{7,5},{8,10},{9,11},{10,... | collective-permute-start | bytes 36872 | tf_op jit(solution)/shard_map/ppermute | solution.py:693
  234.7 5.5 %collective-permute-start.5 = (f32[3,1024]{1,0:T(4,128)S(1)}, f32[3,1024]{1,0:T(4,128)S(1)}, u32[]{:S(2)}, u32[]{:S(2)}) collective-permute-start(f32[3,1024]{1,0:T(4,128)S(1)} %add.290), channel_id=1, source_target_pairs={{0,3},{1,2},{2,1},{3,0},{4,7},{5,6},{6,5},{7,4},{8,11},{9,10},{10,... | collective-permute-start | bytes 36872 | tf_op jit(solution)/shard_map/ppermute | solution.py:693

commit v5 on v4

--- a/solution.py
+++ b/solution.py
@@ -198,7 +198,7 @@
 OUTER = 32
 HALF = LANES // 2
 SUB = LANES // 4
-BATCH = 4
+BATCH = 8
 GROUPS = 16
 LOWS = 64
 
@@ -622,15 +622,12 @@
     slots = lax.iota(jnp.int32, HALF)
     zero = (fam == 0).astype(jnp.int32)
     total = None
-    before = got_bins
     for number, piece in enumerate(pieces):
         chunk, half_chunk = number // 2, number % 2
-        piece, before = lax.optimization_barrier((piece, before))
         got = lax.all_to_all(
             piece, ("rows", "rep"), split_axis=0, concat_axis=0, tiled=True,
             axis_index_groups=groups,
         )
-        before = got
         got = got.reshape(slabs, 2, -1, count // 2, LANES)
         subs = got.shape[2]
         first_col = OUTER * slots if chunk == 0 else OUTER // 2 + OUTER * (HALF - 1 - slots)
@@ -687,14 +684,12 @@
     factors = jnp.array([auto, auto, cross], jnp.float32)[:, None]
     own = summed(partial_sums, "rows")
 
-    def from_rep(shift):
-        if shift == 0:
-            return own
-        return lax.ppermute(own, "rep", [(i, i ^ shift) for i in range(reps)])
-
-    skies = [
-        (from_rep(2 * shift) + from_rep(2 * shift + 1)) * factors for shift in range(reps // 2)
-    ]
+    own = (own + partner(own, "rep", 0)) * factors
+    skies = [own]
+    distance = 1
+    while 1 << distance < reps:
+        skies = skies + [partner(sky, "rep", distance) for sky in skies]
+        distance += 1
     stacked = jnp.stack(skies)
     order = lax.iota(jnp.int32, len(skies)) ^ (member // 2)
     return jnp.take(stacked, order, axis=0) if len(skies) > 2 else jnp.where(

time: 242 us -> 235 us (0.971)
  Pallas kernels: 111 us -> 105 us
    pallas_call x4, Pallas kernels: 72.4 us -> 66.5 us  [on_device_fast(): out = band_call(info, got, got_bins, got_bins, spin, col_high, col_low, fx)]
    ppermute x3 -> x0, waiting for transfers between devices: 5.53 us -> none  [from_rep(): return lax.ppermute(own, 'rep', [(i, i ^ shift) for i in range(reps)])]
    ppermute x3 -> x0, starting transfers between devices: 4.74 us -> none  [from_rep(): return lax.ppermute(own, 'rep', [(i, i ^ shift) for i in range(reps)])]
    ppermute x3 -> x5, starting transfers between devices: 3.27 us -> 8 us  [partner(): lax.ppermute(array, axis, [(i, i ^ 1 << distance) for i in range(lax.axis...]
    ppermute x3 -> x5, waiting for transfers between devices: 5.45 us -> 9.36 us  [partner(): lax.ppermute(array, axis, [(i, i ^ 1 << distance) for i in range(lax.axis...]
  transfers between devices with their start and end apart: 10 -> 9, of which waited for: 8 -> 8; matrix products, arithmetic and copies ran while one was open for 4% -> 4% of each run, Pallas kernels for 34% -> 33%
where the time goes in v5:
time: 235 us
  Pallas kernels  105 us (45%)
  waiting for transfers between devices  60.6 us (26%)
  blocking collectives  30.2 us (13%)
  starting transfers between devices  26.2 us (11%)
  local copies, waits for them, and re-layouts  8.76 us (4%)
  other arithmetic  3.66 us (2%)
    pallas_call x4, Pallas kernels, on_device_fast(): out = band_call(info, got, got_bins, got_bins, spin, col_high, col_low, fx)  66.5 us
    all_to_all x1, blocking collectives, on_device_fast(): lax.all_to_all(piece, ('rows', 'rep'), split_axis=0, concat_axis=0, tiled...  30.2 us
    all_to_all x3, waiting for transfers between devices, on_device_fast(): lax.all_to_all(piece, ('rows', 'rep'), split_axis=0, concat_axis=0, tiled...  29.1 us
    pallas_call x1, Pallas kernels, on_device_fast(): pl.pallas_call(row_kernel, grid=(count // block,), in_specs=[pl.BlockSpec...  27 us
    all_to_all x1, waiting for transfers between devices, on_device_fast(): lax.all_to_all(sent_bins, 'rows', split_axis=0, concat_axis=0, tiled=True)  22.2 us
    all_to_all x3, starting transfers between devices, on_device_fast(): lax.all_to_all(piece, ('rows', 'rep'), split_axis=0, concat_axis=0, tiled...  13 us
    pallas_call x1, Pallas kernels, on_device_fast(): pl.pallas_call(bins_kernel, grid=(OUTER // sub,), in_specs=[pl.BlockSpec(...  11.2 us
    ppermute x5, waiting for transfers between devices, partner(): lax.ppermute(array, axis, [(i, i ^ 1 << distance) for i in range(lax.axis...  9.36 us
  transfers between devices with their start and end apart: 9, of which 8 were waited for; matrix products, arithmetic and copies ran while one was open for 4% of the time, Pallas kernels for 33%

profile of v5, /device:TPU:0, one launch (start us, length us, event | category | flops | bytes accessed | tf_op | source)
XLA Modules:
  0.0 234.9 jit_solution(7336610007046973536)
XLA Ops:
  0.6 11.2 %bins_prep.1 = f32[8,2,32,16,128]{4,3,2,1,0:T(8,128)} custom-call(s32[2]{0:T(128)} %pad_add_fusion.1.info_ref, bf16[2,256,128]{2,1,0:T(8,128)(2,1)} %constant.112.clone.flip_ref, s32[128,32,512]{2,1,0:T(8,128)} %bitcast.35, s32[128,32,512]{2,1,0:T(8,128)} %bitcast.36, s32[128,32,512]{2,1,0:T(8,128)} %bitcast.37, s32[128,32,512]{2,1,0:T(8,128)} %bitcast.38), custom_call_target="tpu_custom_call" | custom-call | flops 5000000000 | bytes 12582912 | tf_op jit(solution)/shard_map/bins_prep/pallas_call | solution.py:571
  11.8 5.2 %all-to-all-start.1 = ((f32[8,2,32,16,128]{4,3,2,1,0:T(8,128)}), f32[8,2,32,16,128]{4,3,2,1,0:T(8,128)}, u32[]{:S(2)}, u32[]{:S(2)}) async-start(f32[8,2,32,16,128]{4,3,2,1,0:T(8,128)} %bins_prep.1), calls=%async_computation.1 | async-start | bytes 8388608 | tf_op jit(solution)/shard_map/all_to_all | solution.py:588
  17.0 27.0 %row_fft.1 = (f32[16,256,128]{2,1,0:T(8,128)}, f32[16,256,128]{2,1,0:T(8,128)}, f32[16,256,128]{2,1,0:T(8,128)}, f32[16,256,128]{2,1,0:T(8,128)}) custom-call(f32[1,512,4096]{2,1,0:T(8,128)} %map_ref.1, s32[512,4096]{1,0:T(8,128)} %mask_ref.1, f32[2,16,128]{2,1,0:T(8,128)} %constant.113.clone.turn_ref, bf16[2,256,256]{2,1,0:T(8,128)(2,1)} %constant.118.high_ref, ...), custom_call_target="tpu_custom_call" | custom-call | flops 12000000000 | bytes 25165824 | tf_op jit(solution)/shard_map/row_fft/pallas_call | solution.py:597
  43.9 22.2 %all-to-all-done.1.bins0_ref.bins1_ref = f32[8,2,32,16,128]{4,3,2,1,0:T(8,128)} async-done(((f32[8,2,32,16,128]{4,3,2,1,0:T(8,128)}), f32[8,2,32,16,128]{4,3,2,1,0:T(8,128)}, u32[]{:S(2)}, u32[]{:S(2)}) %all-to-all-start.1) | async-done | bytes 4194336 | tf_op jit(solution)/shard_map/all_to_all | solution.py:588
  66.2 30.2 %all_to_all.25 = f32[16,256,128]{2,1,0:T(8,128)} all-to-all(f32[16,256,128]{2,1,0:T(8,128)} %get-tuple-element.13), channel_id=1, replica_groups={{0,1,4,5,8,9,12,13,16,17,20,21,24,25,28,29},{2,3,6,7,10,11,14,15,18,19,..., dimensions={0} | all-to-all | bytes 4194304 | tf_op jit(solution)/shard_map/all_to_all | solution.py:627
  96.4 3.7 %all-to-all-start.3 = ((f32[16,256,128]{2,1,0:T(8,128)}), f32[16,256,128]{2,1,0:T(8,128)S(1)}, u32[]{:S(2)}, u32[]{:S(2)}) async-start(f32[16,256,128]{2,1,0:T(8,128)} %get-tuple-element.18), calls=%async_computation.3 | async-start | bytes 4194304 | tf_op jit(solution)/shard_map/all_to_all | solution.py:627
  103.9 23.5 %all-to-all-done.3 = f32[16,256,128]{2,1,0:T(8,128)S(1)} async-done(((f32[16,256,128]{2,1,0:T(8,128)}), f32[16,256,128]{2,1,0:T(8,128)S(1)}, u32[]{:S(2)}, u32[]{:S(2)}) %all-to-all-start.3) | async-done | bytes 2097184 | tf_op jit(solution)/shard_map/all_to_all | solution.py:627
  127.4 4.7 %all-to-all-start.4 = ((f32[16,256,128]{2,1,0:T(8,128)}), f32[16,256,128]{2,1,0:T(8,128)}, u32[]{:S(2)}, u32[]{:S(2)}) async-start(f32[16,256,128]{2,1,0:T(8,128)} %get-tuple-element.19), calls=%async_computation.4 | async-start | bytes 4194304 | tf_op jit(solution)/shard_map/all_to_all | solution.py:627
  132.2 1.6 copy-done
  133.8 16.3 %band_sums.4 = (f32[1,48,64]{2,1,0:T(8,128)S(1)}, f32[1,32,2,256]{3,2,1,0:T(2,128)S(1)}) custom-call(s32[3]{0:T(128)S(1)} %pad_add_fusion.info_ref, f32[8,2,1,256,128]{4,3,2,1,0:T(8,128)S(1)} %bitcast.33, f32[8,2,32,16,128]{4,3,2,1,0:T(8,128)} %all-to-all-done.1.bins0_ref.bins1_ref, f32[8,2,32,16,128]{4,3,2,1,0:T(8,128)} %all-to-all-done.1.bins0_ref.bins1_ref, ...), custom_call_target="tpu_custom_call" | custom-call | flops 10000000000 | bytes 4194304 | tf_op jit(solution)/shard_map/band_sums/pallas_call | solution.py:673
  150.5 2.9 %reverse.5 = f32[2,2,4096]{2,1,0:T(2,128)S(1)} reverse(f32[2,2,4096]{2,1,0:T(2,128)S(1)} %bitcast.41), dimensions={2} | reverse | bytes 131072
  154.3 5.5 %all-to-all-done.4 = f32[16,256,128]{2,1,0:T(8,128)} async-done(((f32[16,256,128]{2,1,0:T(8,128)}), f32[16,256,128]{2,1,0:T(8,128)}, u32[]{:S(2)}, u32[]{:S(2)}) %all-to-all-start.4) | async-done | bytes 2097184 | tf_op jit(solution)/shard_map/all_to_all | solution.py:627
  159.8 4.6 %all-to-all-start.2 = ((f32[16,256,128]{2,1,0:T(8,128)}), f32[16,256,128]{2,1,0:T(8,128)}, u32[]{:S(2)}, u32[]{:S(2)}) async-start(f32[16,256,128]{2,1,0:T(8,128)} %get-tuple-element.17), calls=%async_computation.2 | async-start | bytes 4194304 | tf_op jit(solution)/shard_map/all_to_all | solution.py:627
  166.3 16.3 %band_sums.6 = f32[1,48,64]{2,1,0:T(8,128)S(1)} custom-call(s32[3]{0:T(128)S(1)} %pad_add_fusion.2.info_ref, f32[8,2,1,256,128]{4,3,2,1,0:T(8,128)S(1)} %bitcast.32, f32[8,2,32,16,128]{4,3,2,1,0:T(8,128)} %all-to-all-done.1.bins0_ref.bins1_ref, f32[8,2,32,16,128]{4,3,2,1,0:T(8,128)} %all-to-all-done.1.bins0_ref.bins1_ref, f32[2,64,128]{2,1,0:T(8,128)S(1)} %copy-done.3, ...), custom_call_target="tpu_custom_call" | custom-call | flops 10000000000 | bytes 4194304 | tf_op jit(solution)/shard_map/band_sums/pallas_call | solution.py:673
  182.7 16.9 %band_sums.7 = f32[1,48,64]{2,1,0:T(8,128)S(1)} custom-call(s32[3]{0:T(128)S(1)} %pad_add_fusion.2.info_ref, f32[8,2,1,256,128]{4,3,2,1,0:T(8,128)} %bitcast.18.x_ref, f32[8,2,32,16,128]{4,3,2,1,0:T(8,128)} %all-to-all-done.1.bins0_ref.bins1_ref, f32[8,2,32,16,128]{4,3,2,1,0:T(8,128)} %all-to-all-done.1.bins0_ref.bins1_ref, f32[2,64,128]{2,1,0:T(8,128)S(1)} %copy-done.3, ...), custom_call_target="tpu_custom_call" | custom-call | flops 10000000000 | bytes 4194304 | tf_op jit(solution)/shard_map/band_sums/pallas_call | solution.py:673
  199.7 17.0 %band_sums.5 = f32[1,48,64]{2,1,0:T(8,128)S(1)} custom-call(s32[3]{0:T(128)S(1)} %pad_add_fusion.info_ref, f32[8,2,1,256,128]{4,3,2,1,0:T(8,128)} %bitcast.15.x_ref, f32[8,2,32,16,128]{4,3,2,1,0:T(8,128)} %all-to-all-done.1.bins0_ref.bins1_ref, f32[8,2,32,16,128]{4,3,2,1,0:T(8,128)} %all-to-all-done.1.bins0_ref.bins1_ref, f32[2,64,128]{2,1,0:T(8,128)S(1)} %copy-done.3, ...), custom_call_target="tpu_custom_call" | custom-call | flops 10000000000 | bytes 4194304 | tf_op jit(solution)/shard_map/band_sums/pallas_call | solution.py:673
  218.0 1.6 collective-permute-start.1
  219.6 2.2 collective-permute-done.1
  221.8 1.6 collective-permute-start.2
  223.4 2.1 collective-permute-done.2
  225.5 1.6 collective-permute-start.3
  227.1 2.2 collective-permute-done.3
  229.3 3.2 %collective-permute-start.4 = (f32[3,1024]{1,0:T(4,128)S(1)}, f32[3,1024]{1,0:T(4,128)S(1)}, u32[]{:S(2)}, u32[]{:S(2)}) collective-permute-start(f32[3,1024]{1,0:T(4,128)S(1)} %add_multiply_fusion), channel_id=1, source_target_pairs={{0,2},{1,3},{2,0},{3,1},{4,6},{5,7},{6,4},{7,5},{8,10},{9,11},{10,... | collective-permute-start | bytes 36872 | tf_op jit(solution)/shard_map/ppermute | solution.py:20
  232.5 1.7 collective-permute-done.4
  (69 shorter events, 9.7 us)
Async XLA Ops:
  11.8 54.4 %all-to-all-start.1 = ((f32[8,2,32,16,128]{4,3,2,1,0:T(8,128)}), f32[8,2,32,16,128]{4,3,2,1,0:T(8,128)}, u32[]{:S(2)}, u32[]{:S(2)}) async-start(f32[8,2,32,16,128]{4,3,2,1,0:T(8,128)} %bins_prep.1), calls=%async_computation.1 | async-start | bytes 8388608 | tf_op jit(solution)/shard_map/all_to_all | solution.py:588
  96.4 31.0 %all-to-all-start.3 = ((f32[16,256,128]{2,1,0:T(8,128)}), f32[16,256,128]{2,1,0:T(8,128)S(1)}, u32[]{:S(2)}, u32[]{:S(2)}) async-start(f32[16,256,128]{2,1,0:T(8,128)} %get-tuple-element.18), calls=%async_computation.3 | async-start | bytes 4194304 | tf_op jit(solution)/shard_map/all_to_all | solution.py:627
  127.4 4.7 %copy-start.1 = (bf16[256,256]{1,0:T(8,128)(2,1)S(1)}, bf16[256,256]{1,0:T(8,128)(2,1)}, u32[]{:S(2)}) copy-start(bf16[256,256]{1,0:T(8,128)(2,1)} %constant.122.high_ref) | copy-start | bytes 393220
  127.4 4.7 %copy-start.2 = (bf16[256,256]{1,0:T(8,128)(2,1)S(1)}, bf16[256,256]{1,0:T(8,128)(2,1)}, u32[]{:S(2)}) copy-start(bf16[256,256]{1,0:T(8,128)(2,1)} %constant.125.low_ref) | copy-start | bytes 393220
  127.4 4.7 %copy-start.3 = (f32[2,64,128]{2,1,0:T(8,128)S(1)}, f32[2,64,128]{2,1,0:T(8,128)}, u32[]{:S(2)}) copy-start(f32[2,64,128]{2,1,0:T(8,128)} %constant.114.clone.turn_ref) | copy-start | bytes 196612
  127.4 32.4 %all-to-all-start.4 = ((f32[16,256,128]{2,1,0:T(8,128)}), f32[16,256,128]{2,1,0:T(8,128)}, u32[]{:S(2)}, u32[]{:S(2)}) async-start(f32[16,256,128]{2,1,0:T(8,128)} %get-tuple-element.19), calls=%async_computation.4 | async-start | bytes 4194304 | tf_op jit(solution)/shard_map/all_to_all | solution.py:627
  132.2 1.6 copy-start
  133.8 20.1 %copy-start.4 = (f32[2]{0:T(128)S(1)}, f32[2]{0:T(128)}, u32[]{:S(2)}) copy-start(f32[2]{0:T(128)} %constant.126) | copy-start | bytes 28
  133.8 20.1 %copy-start.5 = (f32[2]{0:T(128)S(1)}, f32[2]{0:T(128)}, u32[]{:S(2)}) copy-start(f32[2]{0:T(128)} %constant.127) | copy-start | bytes 28
  159.8 39.8 %all-to-all-start.2 = ((f32[16,256,128]{2,1,0:T(8,128)}), f32[16,256,128]{2,1,0:T(8,128)}, u32[]{:S(2)}, u32[]{:S(2)}) async-start(f32[16,256,128]{2,1,0:T(8,128)} %get-tuple-element.17), calls=%async_computation.2 | async-start | bytes 4194304 | tf_op jit(solution)/shard_map/all_to_all | solution.py:627
  199.7 29.6 %copy-start.6 = (f32[3]{0:T(128)S(1)}, f32[3]{0:T(128)}, u32[]{:S(2)}) copy-start(f32[3]{0:T(128)} %constant.116.clone) | copy-start | bytes 40
  216.8 1.2 collective-permute-start
  218.0 3.7 %collective-permute-start.1 = (f32[3,1024]{1,0:T(4,128)S(1)}, f32[3,1024]{1,0:T(4,128)S(1)}, u32[]{:S(2)}, u32[]{:S(2)}) collective-permute-start(f32[3,1024]{1,0:T(4,128)S(1)} %add.285), channel_id=1, source_target_pairs={{0,8},{4,12},{8,0},{12,4},{16,24},{20,28},{24,16},{28,20},{1,9},{5... | collective-permute-start | bytes 36872 | tf_op jit(solution)/shard_map/ppermute | solution.py:20
  221.8 3.7 %collective-permute-start.2 = (f32[3,1024]{1,0:T(4,128)S(1)}, f32[3,1024]{1,0:T(4,128)S(1)}, u32[]{:S(2)}, u32[]{:S(2)}) collective-permute-start(f32[3,1024]{1,0:T(4,128)S(1)} %add.286), channel_id=1, source_target_pairs={{0,16},{4,20},{8,24},{12,28},{16,0},{20,4},{24,8},{28,12},{1,17},{... | collective-permute-start | bytes 36872 | tf_op jit(solution)/shard_map/ppermute | solution.py:20
  225.5 3.7 %collective-permute-start.3 = (f32[3,1024]{1,0:T(4,128)S(1)}, f32[3,1024]{1,0:T(4,128)S(1)}, u32[]{:S(2)}, u32[]{:S(2)}) collective-permute-start(f32[3,1024]{1,0:T(4,128)S(1)} %add.287), channel_id=1, source_target_pairs={{0,1},{1,0},{2,3},{3,2},{4,5},{5,4},{6,7},{7,6},{8,9},{9,8},{10,11... | collective-permute-start | bytes 36872 | tf_op jit(solution)/shard_map/ppermute | solution.py:20
  229.3 4.9 %collective-permute-start.4 = (f32[3,1024]{1,0:T(4,128)S(1)}, f32[3,1024]{1,0:T(4,128)S(1)}, u32[]{:S(2)}, u32[]{:S(2)}) collective-permute-start(f32[3,1024]{1,0:T(4,128)S(1)} %add_multiply_fusion), channel_id=1, source_target_pairs={{0,2},{1,3},{2,0},{3,1},{4,6},{5,7},{6,4},{7,5},{8,10},{9,11},{10,... | collective-permute-start | bytes 36872 | tf_op jit(solution)/shard_map/ppermute | solution.py:20
